TPU v7x, 32 devices: a whole 2x2x4 slice. The times are simulated.
32 devices in a mesh: seq: 8 (over z, x), mp: 4 (over y, core).
Axes of the slice: x: 2, y: 2, z: 4, core: 2. Of those that a mesh axis runs over, the one named last changes fastest.
Arguments:
- tokens: bfloat16 [256, 3584], P('mp'), may hold values from -6 to 6
- gain_attn: float32 [3584], replicated, may hold values from 0.25 to 1.75
- w_query: bfloat16 [3584, 3584], P(None, 'seq'), may hold values from -0.09375 to 0.09375
- query_bias: float32 [3584], P('seq'), may hold values from -3 to 3
- cache_keys: bfloat16 [4, 8192, 128], P(None, 'seq'), may hold values from -80 to 80
- cache_values: bfloat16 [4, 8192, 128], P(None, 'seq'), may hold values from -6 to 6
- w_out: bfloat16 [3584, 3584], P(None, 'seq'), may hold values from -0.09375 to 0.09375
- gain_ffn: float32 [3584], P('seq'), may hold values from 0.25 to 1.75
- w_gate: bfloat16 [3584, 18944], P('mp', 'seq'), may hold values from -0.09375 to 0.09375
- w_up: bfloat16 [3584, 18944], P('mp', 'seq'), may hold values from -0.09375 to 0.09375
- w_down: bfloat16 [18944, 3584], P('seq', 'mp'), may hold values from -0.0625 to 0.0625
Outputs:
- attended: bfloat16 [256, 3584], P('mp', 'seq')
- layer_out: bfloat16 [256, 3584], P('mp', 'seq')
All inputs are finite; a program needn't handle non-finite values.
Results may differ from a plain program's by a relative error of at most 0.012.
The roundings to bfloat16 on the way count: a program that leaves them out, or rounds other values in their place, can miss the bound.
Values may be sent and summed in bfloat16 or wider, within the bound.
A program may use at most 64 MiB of HBM per device.

v0:
```python
import functools

import jax
import jax.numpy as jnp
from jax import lax
from jax.experimental import pallas as pl
from jax.experimental.pallas import tpu as pltpu
from jax.sharding import PartitionSpec as P

D = 3584
HEADS = 28
KV_HEADS = 4
HEAD = 128
GROUP = HEADS // KV_HEADS
SUM_ROW = 8
CHUNKS = 2
HALVES = 2

eps = 1e-06
MESH = pl.DeviceIdType.MESH
VMEM = pltpu.VMEM


class SeqPlan:
    def __init__(self, n_seq, n_mp):
        self.count = n_seq

    def dest(self, s, m, i):
        to = lax.rem(s + i, self.count)
        return to, m, to

    def my_slot(self, s, m):
        return s

    def source(self, s, m, i):
        return i, m


class StatPlan(SeqPlan):
    def dest(self, s, m, i):
        to = lax.rem(s + i, self.count)
        return to, m, to // (self.count // KV_HEADS)


class RowsPlan:
    def __init__(self, n_seq, n_mp):
        self.count, self.per = n_seq, n_seq // n_mp

    def dest(self, s, m, i):
        to = lax.rem(s + i, self.count)
        return to, s // self.per, to

    def my_slot(self, s, m):
        return m * self.per + lax.rem(s, self.per)

    def source(self, s, m, i):
        return m * self.per + i % self.per, i // self.per


class HomePlan:
    def __init__(self, n_seq, n_mp):
        self.count, self.per, self.n_mp = n_seq, n_seq // n_mp, n_mp

    def dest(self, s, m, i):
        to_m = lax.rem(m + i // self.per, self.n_mp)
        j = lax.rem(s + i, self.per)
        return m * self.per + j, to_m, to_m * self.per + j

    def my_slot(self, s, m):
        return s

    def source(self, s, m, i):
        return i, s // self.per


def greet(plans, s, m):
    barrier = pltpu.get_barrier_semaphore()
    total = 0
    for plan in plans:
        for i in range(plan.count):
            pl.semaphore_signal(
                barrier, inc=1, device_id=plan.source(s, m, i), device_id_type=MESH
            )
        total += plan.count
    pl.semaphore_wait(barrier, total)


def push(src, dst, send, recv, to):
    return pltpu.make_async_remote_copy(
        src_ref=src,
        dst_ref=dst,
        send_sem=send,
        recv_sem=recv,
        device_id=to,
        device_id_type=MESH,
    )


class Flow:
    def __init__(self, plan, src, dst, spread, send, recv, s, m):
        self.plan, self.src, self.dst, self.spread = plan, src, dst, spread
        self.send, self.recv, self.s, self.m = send, recv, s, m
        self.started = []

    def start(self, i):
        to_s, to_m, index = self.plan.dest(self.s, self.m, i)
        mine = self.plan.my_slot(self.s, self.m)
        block = self.src.at[index] if self.spread else self.src
        here = jnp.logical_and(to_s == self.s, to_m == self.m)
        remote = push(block, self.dst.at[mine], self.send.at[i], self.recv.at[mine], (to_s, to_m))
        local = pltpu.make_async_copy(block, self.dst.at[mine], self.send.at[i])

        @pl.when(here)
        def _():
            local.start()

        @pl.when(jnp.logical_not(here))
        def _():
            remote.start()

        self.started.append((here, local, remote))

    def arrive(self):
        for i in range(self.plan.count):
            from_s, from_m = self.plan.source(self.s, self.m, i)
            block = self.src.at[0] if self.spread else self.src
            copy = push(block, self.dst.at[i], self.recv.at[i], self.recv.at[i], (from_s, from_m))

            @pl.when(jnp.logical_not(jnp.logical_and(from_s == self.s, from_m == self.m)))
            def _():
                copy.wait_recv()

        for here, local, remote in self.started:

            @pl.when(here)
            def _():
                local.wait()

    def left(self):
        for here, local, remote in self.started:

            @pl.when(jnp.logical_not(here))
            def _():
                remote.wait_send()


def exchange_kernel(plans, spread, *refs):
    k = len(plans)
    ins, outs, sems = refs[:k], refs[k : 2 * k], refs[2 * k :]
    s, m = lax.axis_index("seq"), lax.axis_index("mp")
    greet(list({type(plan): plan for plan in plans}.values()), s, m)
    flows = [
        Flow(plans[a], ins[a], outs[a], spread[a], sems[2 * a], sems[2 * a + 1], s, m)
        for a in range(k)
    ]
    for i in range(max(plan.count for plan in plans)):
        for flow in flows:
            if i < flow.plan.count:
                flow.start(i)
    for flow in flows:
        flow.arrive()
    for flow in flows:
        flow.left()


def exchange(name, cid, *items):
    plans = [item[0] for item in items]
    arrays = [item[1] for item in items]
    spread = [item[2] for item in items]
    shapes = []
    sems = []
    for plan, array, one_each in items:
        block = array.shape[1:] if one_each else array.shape
        shapes.append(jax.ShapeDtypeStruct((plan.count,) + block, array.dtype))
        sems += [pltpu.SemaphoreType.DMA((plan.count,))] * 2
    return pl.pallas_call(
        functools.partial(exchange_kernel, plans, spread),
        out_shape=tuple(shapes),
        in_specs=[pl.BlockSpec(memory_space=VMEM)] * len(items),
        out_specs=tuple([pl.BlockSpec(memory_space=VMEM)] * len(items)),
        scratch_shapes=sems,
        compiler_params=pltpu.CompilerParams(collective_id=cid, has_side_effects=True),
        name=name,
    )(*arrays)


def gather_kernel(n, src, out, sems):
    s, m = lax.axis_index("seq"), lax.axis_index("mp")
    half = n // 2
    hi, lo = s // 2, lax.rem(s, 2)
    partner = (hi * 2 + 1 - lo, m)
    barrier = pltpu.get_barrier_semaphore()
    peers = [lax.rem(hi + d, half) * 2 + lo for d in range(half)]
    for peer in peers[1:]:
        pl.semaphore_signal(barrier, inc=1, device_id=(peer, m), device_id_type=MESH)
    pl.semaphore_signal(barrier, inc=1, device_id=partner, device_id_type=MESH)
    pl.semaphore_wait(barrier, half)
    own = pltpu.make_async_copy(src, out.at[s], sems.at[4, 0])
    own.start()
    direct = [
        push(src, out.at[s], sems.at[0, d], sems.at[1, d], (peers[d], m)) for d in range(1, half)
    ]
    for copy in direct:
        copy.start()
    handed = [push(src, out.at[s], sems.at[2, 0], sems.at[3, 0], partner)]
    handed[0].start()
    for d in range(1, half):
        direct[d - 1].wait_recv()
        at = lax.rem(hi + half - d, half) * 2 + lo
        copy = push(out.at[at], out.at[at], sems.at[2, d], sems.at[3, d], partner)
        copy.start()
        handed.append(copy)
    for copy in handed:
        copy.wait_recv()
    own.wait()
    for copy in direct + handed:
        copy.wait_send()


def gather(name, cid, n, block):
    vmem = pl.BlockSpec(memory_space=VMEM)
    return pl.pallas_call(
        functools.partial(gather_kernel, n),
        out_shape=jax.ShapeDtypeStruct((n,) + block.shape, block.dtype),
        in_specs=[vmem],
        out_specs=vmem,
        scratch_shapes=[pltpu.SemaphoreType.DMA((5, n // 2))],
        compiler_params=pltpu.CompilerParams(collective_id=cid, has_side_effects=True),
        name=name,
    )(block)


def attention_kernel(q_ref, k_ref, v_ref, out_ref, stat_ref):
    count, rows, width = q_ref.shape
    q = jnp.concatenate([q_ref[j] for j in range(count)], axis=1)
    stacked = jnp.concatenate([q[:, h * HEAD : (h + 1) * HEAD] for h in range(GROUP)], axis=0)
    scores = times_transposed(stacked, k_ref[0]) * HEAD ** (-0.5)
    highest = jnp.max(scores, axis=1, keepdims=True)
    probs = jnp.exp(scores - highest)
    sums = jnp.sum(probs, axis=1, keepdims=True)
    weighted = jnp.dot(probs.astype(jnp.bfloat16), v_ref[0], preferred_element_type=jnp.float32)
    side = jnp.concatenate([weighted[h * rows : (h + 1) * rows] for h in range(GROUP)], axis=1)
    for j in range(count):
        out_ref[j] = side[:, j * width : (j + 1) * width].astype(jnp.bfloat16)
    stat_ref[...] = jnp.zeros_like(stat_ref)
    for h in range(GROUP):
        part = slice(h * rows, (h + 1) * rows)
        stat_ref[0, h : h + 1, :] = column_to_row(highest[part])
        stat_ref[0, h + SUM_ROW : h + SUM_ROW + 1, :] = column_to_row(sums[part])


def attention(queries, keys, values):
    n, rows, width = queries.shape
    context = keys.shape[1]
    count = n // KV_HEADS
    blocks = pl.BlockSpec((count, rows, width), lambda g: (g, 0, 0))
    cache = pl.BlockSpec((1, context, HEAD), lambda g: (g, 0, 0))
    return pl.pallas_call(
        attention_kernel,
        grid=(KV_HEADS,),
        out_shape=(
            jax.ShapeDtypeStruct((n, rows, width), jnp.bfloat16),
            jax.ShapeDtypeStruct((KV_HEADS, 2 * SUM_ROW, rows), jnp.float32),
        ),
        in_specs=[blocks, cache, cache],
        out_specs=(blocks, pl.BlockSpec((1, 2 * SUM_ROW, rows), lambda g: (g, 0, 0))),
        name="block_attention",
    )(queries, keys, values)


def merge_kernel(weighted_ref, stat_ref, out_ref):
    n, rows, width = weighted_ref.shape
    s = lax.axis_index("seq")
    maxima, sums = stat_ref[:, :SUM_ROW, :], stat_ref[:, SUM_ROW:, :]
    rescale = jnp.exp(maxima - jnp.max(maxima, axis=0, keepdims=True))
    total = jnp.sum(sums * rescale, axis=0)
    row = lax.broadcasted_iota(jnp.int32, (SUM_ROW, rows), 0)
    inverse = 1.0 / jnp.where(row < GROUP, total, 1.0)
    shape = (SUM_ROW, width)
    column = s * width + lax.broadcasted_iota(jnp.int32, shape, 1)
    head = lax.div(column, HEAD) - s // (n // KV_HEADS) * GROUP
    pick = jnp.where(head == lax.broadcasted_iota(jnp.int32, shape, 0), 1.0, 0.0)
    result = jnp.zeros((rows, width), jnp.float32)
    for j in range(n):
        factor = lax.dot_general(
            rescale[j] * inverse,
            pick,
            (((0,), (0,)), ((), ())),
            precision=lax.Precision.HIGHEST,
            preferred_element_type=jnp.float32,
        )
        result = result + weighted_ref[j].astype(jnp.float32) * factor
    out_ref[...] = result.astype(jnp.bfloat16)


def project_kernel(blocks, w_out, own_tokens, gain, residual, scaled, square):
    attended = jnp.concatenate([blocks[j] for j in range(blocks.shape[0])], axis=1)
    total = own_tokens[...] + times_transposed(attended, w_out[...])
    residual[...] = total
    scaled[...] = (total * gain[...]).astype(jnp.bfloat16)
    square[...] = column_to_row(jnp.sum(total * total, axis=1, keepdims=True))


def simple(kernel, out_shape, *arrays):
    return pl.pallas_call(kernel, out_shape=out_shape, name=kernel.__name__)(*arrays)


def times_transposed(a, b):
    return lax.dot_general(a, b, (((1,), (1,)), ((), ())), preferred_element_type=jnp.float32)


def row_to_column(row):
    k = row.shape[1]
    across = lax.broadcasted_iota(jnp.int32, (k, k), 1)
    down = lax.broadcasted_iota(jnp.int32, (k, k), 0)
    return jnp.sum(jnp.where(across == down, row, 0.0), axis=1, keepdims=True)


def column_to_row(column):
    k = column.shape[0]
    across = lax.broadcasted_iota(jnp.int32, (k, k), 1)
    down = lax.broadcasted_iota(jnp.int32, (k, k), 0)
    return jnp.sum(jnp.where(across == down, column, 0.0), axis=0, keepdims=True)


def ffn_kernel(plans, bounds, *refs):
    seq, to_rows, home = plans
    scaled, square, residual, gate_hbm, up_hbm, down_hbm, out = refs[:7]
    refs = refs[7:]
    gate_w, up_w, down_w, blocks, squares, features, acc, down_out, terms = refs[:9]
    refs = refs[9:]
    w_sems, sems = refs[0], refs[1 : 3 + 4 * HALVES]
    c_sems = refs[3 + 4 * HALVES]
    chunk_refs = refs[4 + 4 * HALVES :]
    s, m = lax.axis_index("seq"), lax.axis_index("mp")
    core, y = lax.rem(m, 2), m // 2
    sibling = (s, y * 2 + (1 - core))
    across = (s, (1 - y) * 2 + core)
    rows, width = scaled.shape[0] // HALVES, scaled.shape[1]
    per, n_mp = to_rows.per, home.n_mp
    loads = [
        pltpu.make_async_copy(gate_hbm, gate_w, w_sems.at[0]),
        pltpu.make_async_copy(up_hbm, up_w, w_sems.at[1]),
        pltpu.make_async_copy(down_hbm, down_w, w_sems.at[2]),
    ]
    for load in loads:
        load.start()
    barrier = pltpu.get_barrier_semaphore()
    for peer in (sibling, across):
        pl.semaphore_signal(barrier, inc=1, device_id=peer, device_id_type=MESH)
    for plan in plans:
        for i in range(plan.count):
            pl.semaphore_signal(
                barrier, inc=1, device_id=plan.source(s, m, i), device_id_type=MESH
            )
    pl.semaphore_wait(barrier, 2 + sum(plan.count for plan in plans))
    mains = [
        Flow(
            to_rows, scaled.at[pl.ds(h * rows, rows)], blocks.at[h], False,
            sems[2 + 4 * h], sems[3 + 4 * h], s, m,
        )
        for h in range(HALVES)
    ]
    side = Flow(seq, square, squares, False, sems[0], sems[1], s, m)
    for main in mains:
        for i in range(to_rows.count):
            main.start(i)
    for i in range(seq.count):
        side.start(i)
    order = (1 - core, 3 - core, core, 2 + core)

    def collect(h):
        mains[h].arrive()
        for p, t in enumerate(order):
            features[h, p * rows : (p + 1) * rows, :] = jnp.concatenate(
                [blocks[h, t * per + j] for j in range(per)], axis=1
            )

    chunks = []
    for c, (h, first, last) in enumerate(bounds):
        kept, s1_out, s1_in, s2_out, s2_in, act = chunk_refs[6 * c : 6 * c + 6]
        sem = lambda k, c=c: c_sems.at[c, k]
        chunks.append(
            dict(
                half=h, first=first, last=last, kept=kept, s1_out=s1_out, s1_in=s1_in,
                s2_out=s2_out, s2_in=s2_in, act=act,
                s1=push(s1_out, s1_in, sem(0), sem(1), sibling),
                s2=push(s2_out, s2_in, sem(2), sem(3), across),
                near=push(act.at[m], act.at[m], sem(4), sem(5), sibling),
                far=push(act.at[m], act.at[m], sem(6), sem(7), across),
                relay=push(act.at[across[1]], act.at[across[1]], sem(8), sem(9), sibling),
            )
        )

    def multiply(ch):
        for g, weight in enumerate((gate_w, up_w)):
            part = times_transposed(features[ch["half"]], weight[ch["first"] : ch["last"], :])
            for p in range(2):
                ch["s1_out"][g, p] = part[p * rows : (p + 1) * rows].astype(jnp.bfloat16)
                ch["kept"][g, p] = part[(p + 2) * rows : (p + 3) * rows]
        ch["s1"].start()

    def pair_sum(ch):
        ch["s1"].wait_recv()
        for g in range(2):
            ch["s2_out"][g] = (
                ch["kept"][g, 1 - y] + ch["s1_in"][g, 1 - y].astype(jnp.float32)
            ).astype(jnp.bfloat16)
        ch["s2"].start()

    def activate(ch, inverse):
        ch["s2"].wait_recv()
        total = [
            (
                ch["kept"][g, y]
                + ch["s1_in"][g, y].astype(jnp.float32)
                + ch["s2_in"][g].astype(jnp.float32)
            )
            * inverse
            for g in range(2)
        ]
        gate, up = total
        ch["act"][m] = (gate / (1.0 + jnp.exp(-gate)) * up).astype(jnp.bfloat16)
        ch["far"].start()
        ch["near"].start()

    def finish(h):
        own = halves[h]
        for c, ch in enumerate(own):
            ch["far"].wait_recv()
            ch["relay"].start()
            ch["near"].wait_recv()
            ch["relay"].wait_recv()
            act = ch["act"][...].reshape(n_mp * rows, ch["last"] - ch["first"])
            part = jnp.dot(
                act, down_w[ch["first"] : ch["last"], :], preferred_element_type=jnp.float32
            )
            total = part if c == 0 else acc[...] + part
            if c < len(own) - 1:
                acc[...] = total
        for t in range(n_mp):
            for j in range(per):
                down_out[h, t * per + j] = total[
                    t * rows : (t + 1) * rows, j * width : (j + 1) * width
                ].astype(jnp.bfloat16)
        flow = Flow(
            home, down_out.at[h], terms.at[h], True, sems[4 + 4 * h], sems[5 + 4 * h], s, m
        )
        for i in range(home.count):
            flow.start(i)
        return flow

    halves = [[ch for ch in chunks if ch["half"] == h] for h in range(HALVES)]
    collect(0)
    loads[0].wait()
    loads[1].wait()
    for c, ch in enumerate(halves[0]):
        multiply(ch)
        if c >= 1:
            pair_sum(halves[0][c - 1])
    pair_sum(halves[0][-1])
    side.arrive()
    inverse = row_to_column(lax.rsqrt(jnp.sum(squares[...], axis=0) / D + eps))
    finals = []
    for h in range(1, HALVES):
        collect(h)
        for ch in halves[h]:
            multiply(ch)
        for ch in halves[h - 1]:
            activate(ch, inverse[(h - 1) * rows : h * rows])
        for ch in halves[h]:
            pair_sum(ch)
        if h == 1:
            loads[2].wait()
        finals.append(finish(h - 1))
    for ch in halves[-1]:
        activate(ch, inverse[(HALVES - 1) * rows : HALVES * rows])
    finals.append(finish(HALVES - 1))
    for h, flow in enumerate(finals):
        flow.arrive()
        part = slice(h * rows, (h + 1) * rows)
        result = residual[part, :]
        for i in range(home.count):
            result = result + terms[h, i].astype(jnp.float32)
        out[part, :] = result.astype(jnp.bfloat16)
    for flow in mains + [side] + finals:
        flow.left()
    for ch in chunks:
        for name in ("s1", "s2", "near", "far", "relay"):
            ch[name].wait_send()


def ffn(plans, scaled, square, residual, w_gate, w_up, w_down):
    seq, to_rows, home = plans
    rows, width = scaled.shape
    n_mp, n = home.n_mp, home.count
    hidden = w_gate.shape[0]
    step = max(128, -(-hidden // CHUNKS // 128) * 128)
    bounds = [
        (h, at, min(at + step, hidden))
        for h in range(HALVES)
        for at in range(0, hidden, step)
    ]
    part = rows // HALVES
    bf16, f32 = jnp.bfloat16, jnp.float32
    scratch = [
        VMEM(w_gate.shape, bf16),
        VMEM(w_up.shape, bf16),
        VMEM(w_down.shape, bf16),
        VMEM((HALVES, n, part, width), bf16),
        VMEM((n, 1, rows), f32),
        VMEM((HALVES, n_mp * part, w_gate.shape[1]), bf16),
        VMEM((n_mp * part, w_down.shape[1]), f32),
        VMEM((HALVES, n, part, width), bf16),
        VMEM((HALVES, n, part, width), bf16),
        pltpu.SemaphoreType.DMA((3,)),
    ]
    scratch += [pltpu.SemaphoreType.DMA((n,))] * (2 + 4 * HALVES)
    scratch += [pltpu.SemaphoreType.DMA((len(bounds), 10))]
    for _, first, last in bounds:
        wide = last - first
        scratch += [
            VMEM((2, 2, part, wide), f32),
            VMEM((2, 2, part, wide), bf16),
            VMEM((2, 2, part, wide), bf16),
            VMEM((2, part, wide), bf16),
            VMEM((2, part, wide), bf16),
            VMEM((n_mp, part, wide), bf16),
        ]
    vmem, anywhere = pl.BlockSpec(memory_space=VMEM), pl.BlockSpec(memory_space=pl.ANY)
    return pl.pallas_call(
        functools.partial(ffn_kernel, plans, bounds),
        out_shape=jax.ShapeDtypeStruct((rows, width), bf16),
        in_specs=[vmem] * 3 + [anywhere] * 3,
        out_specs=vmem,
        scratch_shapes=scratch,
        compiler_params=pltpu.CompilerParams(
            collective_id=4, has_side_effects=True, vmem_limit_bytes=60 * 2**20
        ),
        name="ffn",
    )(scaled, square, residual, w_gate, w_up, w_down)


def body(
    n_seq,
    n_mp,
    tokens,
    gain_attn,
    w_query,
    query_bias,
    cache_keys,
    cache_values,
    w_out,
    gain_ffn,
    w_gate,
    w_up,
    w_down,
):
    seq, to_rows, home = (kind(n_seq, n_mp) for kind in (SeqPlan, RowsPlan, HomePlan))
    rows = tokens.shape[0]
    col_width = w_query.shape[1]
    offset = lax.axis_index("seq") * col_width
    hidden_in = tokens.astype(jnp.float32)
    mean_sq = jnp.mean(hidden_in * hidden_in, axis=1, keepdims=True)
    normed = (hidden_in * lax.rsqrt(mean_sq + eps) * gain_attn).astype(jnp.bfloat16)
    query_cols = (jnp.dot(normed, w_query, preferred_element_type=jnp.float32) + query_bias).astype(
        jnp.bfloat16
    )
    query_blocks = gather("queries", 1, n_seq, query_cols)
    weighted, stats = attention(query_blocks, cache_keys, cache_values)
    weighted, stats = exchange(
        "merge", 2, (seq, weighted, True), (StatPlan(n_seq, n_mp), stats, True)
    )
    block = jax.ShapeDtypeStruct((rows, col_width), jnp.bfloat16)
    wide = jax.ShapeDtypeStruct((rows, col_width), jnp.float32)
    attended = simple(merge_kernel, block, weighted, stats)
    attended_blocks = gather("attended", 3, n_seq, attended)
    residual, scaled, square_part = simple(
        project_kernel,
        (wide, block, jax.ShapeDtypeStruct((1, rows), jnp.float32)),
        attended_blocks,
        w_out.T,
        lax.dynamic_slice_in_dim(hidden_in, offset, col_width, 1),
        gain_ffn[None, :],
    )
    layer_out = ffn(
        (seq, to_rows, home), scaled, square_part, residual, w_gate.T, w_up.T, w_down
    )
    return (attended, layer_out)


def solution(mesh):
    placed = (
        P("mp", None),
        P(),
        P(None, "seq"),
        P("seq"),
        P(None, "seq", None),
        P(None, "seq", None),
        P(None, "seq"),
        P("seq"),
        P("mp", "seq"),
        P("mp", "seq"),
        P("seq", "mp"),
    )
    return jax.shard_map(
        functools.partial(body, mesh.shape["seq"], mesh.shape["mp"]),
        mesh=mesh,
        in_specs=placed,
        out_specs=(P("mp", "seq"), P("mp", "seq")),
        check_vma=False,
    )
```

profile of v0, /device:TPU:5, one launch (start us, length us, event | category | flops | bytes accessed | tf_op | source)
XLA Modules:
  0.0 128.7 jit_solution(9084698477852829654)
XLA Ops:
  0.6 0.0 copy-start
  0.7 1.4 %multiply_reduce_fusion = f32[64]{0:T(128)S(1)} fusion(bf16[64,3584]{1,0:T(8,128)(2,1)} %param.11), kind=kLoop, calls=%fused_computation.3 | loop fusion | flops 688064 | bytes 459008 | tf_op jit(solution)/shard_map/reduce_sum | solution.py:564
  2.0 0.7 copy-done
  2.7 2.7 %fusion.src = bf16[64,448]{1,0:T(8,128)(2,1)} fusion(bf16[3584,448]{0,1:T(8,128)(2,1)S(1)} %copy-done, f32[3584]{0:T(1024)} %param.12, f32[64]{0:T(128)S(1)} %add_rsqrt_fusion, bf16[64,3584]{1,0:T(8,128)(2,1)} %param.11, f32[448]{0:T(512)} %param.14), kind=kOutput, calls=%fused_computation.1 | convolution fusion | flops 206495744 | bytes 3743744 | tf_op jit(solution)/shard_map/dot_general | solution.py:566
  5.4 15.3 %queries.1.q_ref = bf16[8,64,448]{2,1,0:T(8,128)(2,1)} custom-call(bf16[64,448]{1,0:T(8,128)(2,1)} %fusion.src), custom_call_target="tpu_custom_call" | custom-call | tf_op jit(solution)/shard_map/queries/pallas_call | solution.py:222
  20.7 7.9 %block_attention.1 = (bf16[8,64,448]{2,1,0:T(8,128)(2,1)}, f32[4,16,64]{2,1,0:T(8,128)}) custom-call(bf16[8,64,448]{2,1,0:T(8,128)(2,1)} %queries.1.q_ref, bf16[4,1024,128]{2,1,0:T(8,128)(2,1)} %k_ref.1, bf16[4,1024,128]{2,1,0:T(8,128)(2,1)} %v_ref.1), custom_call_target="tpu_custom_call" | custom-call | tf_op jit(solution)/shard_map/block_attention/pallas_call | solution.py:258
  28.6 8.7 %merge.1 = (bf16[8,64,448]{2,1,0:T(8,128)(2,1)}, f32[8,16,64]{2,1,0:T(8,128)}) custom-call(bf16[8,64,448]{2,1,0:T(8,128)(2,1)} %get-tuple-element.9.refs_0_, f32[4,16,64]{2,1,0:T(8,128)} %get-tuple-element.10.refs_1_), custom_call_target="tpu_custom_call" | custom-call | tf_op jit(solution)/shard_map/merge/pallas_call | solution.py:176
  37.3 2.7 %merge_kernel.1.src = bf16[64,448]{1,0:T(8,128)(2,1)} custom-call(bf16[8,64,448]{2,1,0:T(8,128)(2,1)} %get-tuple-element.11.weighted_ref, f32[8,16,64]{2,1,0:T(8,128)} %get-tuple-element.12.stat_ref), custom_call_target="tpu_custom_call" | custom-call | tf_op jit(solution)/shard_map/merge_kernel/pallas_call | solution.py:305
  40.0 18.9 %attended.1.blocks = bf16[8,64,448]{2,1,0:T(8,128)(2,1)} custom-call(bf16[64,448]{1,0:T(8,128)(2,1)} %merge_kernel.1.src), custom_call_target="tpu_custom_call" | custom-call | tf_op jit(solution)/shard_map/attended/pallas_call | solution.py:222
  58.9 1.1 convert_element_type.9
  60.0 0.8 constant_dynamic-slice_fusion.own_tokens
  60.8 3.8 %project_kernel.1 = (f32[64,448]{1,0:T(8,128)}, bf16[64,448]{1,0:T(8,128)(2,1)}, f32[1,64]{1,0:T(1,128)}) custom-call(bf16[8,64,448]{2,1,0:T(8,128)(2,1)} %attended.1.blocks, bf16[448,3584]{1,0:T(8,128)(2,1)} %bitcast.7, f32[64,448]{1,0:T(8,128)} %constant_dynamic-slice_fusion.own_tokens, f32[1,448]{1,0:T(1,128)} %bitcast.8), custom_call_target="tpu_custom_call" | custom-call | tf_op jit(solution)/shard_map/project_kernel/pallas_call | solution.py:305
  64.5 62.7 %ffn.1 = bf16[64,448]{1,0:T(8,128)(2,1)} custom-call(bf16[64,448]{1,0:T(8,128)(2,1)} %get-tuple-element.13.refs_0_, f32[1,64]{1,0:T(1,128)} %get-tuple-element.14.refs_1_, f32[64,448]{1,0:T(8,128)} %get-tuple-element.15.refs_2_, bf16[2368,896]{1,0:T(8,128)(2,1)} %bitcast.5, bf16[2368,896]{1,0:T(8,128)(2,1)} %bitcast.6, bf16[2368,896]{1,0:T(8,128)(2,1)} %refs_5_.1), custom_call_target="tpu_custom_call" | custom-call | tf_op jit(solution)/shard_map/ffn/pallas_call | solution.py:531
  127.3 1.5 %copy.14 = bf16[64,448]{1,0:T(8,128)(2,1)} copy(bf16[64,448]{1,0:T(8,128)(2,1)} %ffn.1) | data formatting | bytes 114688
  (1 shorter events, 0.0 us)
Async XLA Ops:
  0.6 2.1 %copy-start = (bf16[3584,448]{0,1:T(8,128)(2,1)S(1)}, bf16[3584,448]{0,1:T(8,128)(2,1)}, u32[]{:S(2)}) copy-start(bf16[3584,448]{0,1:T(8,128)(2,1)} %param.13) | copy-start | bytes 9633796
where the time goes:
time: 131 us; the launch traced here: 129 us
  Pallas kernels  120 us (92%)
  local copies, waits for them, and re-layouts  2.89 us (2%)
  matrix products  2.71 us (2%)
  other arithmetic  2.45 us (2%)
    pallas_call x1, Pallas kernels, ffn(): pl.pallas_call(functools.partial(ffn_kernel, plans, bounds), out_shape=ja...  62.7 us
    pallas_call x2, Pallas kernels, gather(): pl.pallas_call(functools.partial(gather_kernel, n), out_shape=jax.ShapeDt...  34.2 us
    pallas_call x1, Pallas kernels, exchange(): pl.pallas_call(functools.partial(exchange_kernel, plans, spread), out_sha...  8.7 us
    pallas_call x1, Pallas kernels, attention(): pl.pallas_call(attention_kernel, grid=(KV_HEADS,), out_shape=(jax.ShapeDt...  7.88 us
    pallas_call x2, Pallas kernels, simple(): pl.pallas_call(kernel, out_shape=out_shape, name=kernel.__name__)(*arrays)  6.48 us
    dot_general x1, matrix products, body(): jnp.dot(normed, w_query, preferred_element_type=jnp.float32) + query_bias  2.71 us

commit v1 on v0

v1 whole, which is shorter than its diff:
```python
import functools
import math
import types

import jax
import jax.numpy as jnp
from jax import lax
from jax.experimental import pallas as pl
from jax.experimental.pallas import tpu as pltpu
from jax.sharding import PartitionSpec as P

D = 3584
HEADS = 28
KV_HEADS = 4
HEAD = 128
GROUP = HEADS // KV_HEADS
SUM_ROW = 8
CHUNKS = 2
HALVES = 2

eps = 1e-06
EXP2_SCALE = HEAD ** (-0.5) * math.log2(math.e)
MESH = pl.DeviceIdType.MESH
VMEM = pltpu.VMEM
ARGS = (
    "tokens_hbm", "gain_attn_hbm", "w_query_hbm", "bias_hbm", "keys_hbm", "values_hbm",
    "w_out_hbm", "gain_ffn_hbm", "gate_hbm", "up_hbm", "down_hbm",
)
OUTS = ("attended", "out")


def push(src, dst, send, recv, to):
    return pltpu.make_async_remote_copy(
        src_ref=src,
        dst_ref=dst,
        send_sem=send,
        recv_sem=recv,
        device_id=to,
        device_id_type=MESH,
    )


def times_transposed(a, b):
    return lax.dot_general(a, b, (((1,), (1,)), ((), ())), preferred_element_type=jnp.float32)


def row_to_column(row):
    k = row.shape[1]
    across = lax.broadcasted_iota(jnp.int32, (k, k), 1)
    down = lax.broadcasted_iota(jnp.int32, (k, k), 0)
    return jnp.sum(jnp.where(across == down, row, 0.0), axis=1, keepdims=True)


def column_to_row(column):
    k = column.shape[0]
    across = lax.broadcasted_iota(jnp.int32, (k, k), 1)
    down = lax.broadcasted_iota(jnp.int32, (k, k), 0)
    return jnp.sum(jnp.where(across == down, column, 0.0), axis=0, keepdims=True)


class Place:
    def __init__(self, n, n_mp):
        self.n, self.n_mp = n, n_mp
        self.lines, self.per, self.wide = n // 2, n // n_mp, n // KV_HEADS
        self.s, self.m = lax.axis_index("seq"), lax.axis_index("mp")
        self.hi, self.lo = self.s // 2, lax.rem(self.s, 2)
        self.y, self.core = self.m // 2, lax.rem(self.m, 2)
        self.partner = (self.hi * 2 + 1 - self.lo, self.m)
        self.sibling = (self.s, self.y * 2 + (1 - self.core))
        self.across = (self.s, (1 - self.y) * 2 + self.core)

    def ahead(self, d):
        return lax.rem(self.hi + d, self.lines)

    def behind(self, d):
        return lax.rem(self.hi + self.lines - d, self.lines)

    def near(self, b, m):
        return (self.hi * 2 + lax.rem(self.lo + b, 2), m)

    def group(self, j):
        return lax.rem(self.s // self.wide + KV_HEADS - j, KV_HEADS)


def greet(at):
    barrier = pltpu.get_barrier_semaphore()
    peers = [(lax.rem(at.s + d, at.n), at.m) for d in range(1, at.n)]
    peers += [
        at.near(b, lax.rem(at.m + i, at.n_mp)) for i in range(1, at.n_mp) for b in range(2)
    ]
    for peer in peers:
        pl.semaphore_signal(barrier, inc=1, device_id=peer, device_id_type=MESH)
    return lambda: pl.semaphore_wait(barrier, len(peers))


class Gather:
    def __init__(self, at, buf, sems):
        self.at, self.buf, self.sems = at, buf, sems
        self.direct = [
            push(
                buf.at[at.s], buf.at[at.s], sems.at[0, d], sems.at[1, d],
                (at.ahead(d) * 2 + at.lo, at.m),
            )
            for d in range(1, at.lines)
        ]
        self.handed, self.taken = [], 0

    def start(self):
        for copy in self.direct:
            copy.start()
        self.hand(0)

    def hand(self, d):
        at = self.at
        if d < len(self.handed):
            return
        if d:
            self.direct[d - 1].wait_recv()
        block = self.buf.at[at.behind(d) * 2 + at.lo]
        copy = push(block, block, self.sems.at[2, d], self.sems.at[3, d], at.partner)
        copy.start()
        self.handed.append(copy)

    def take(self, j):
        last = j if self.at.lines == KV_HEADS else self.at.lines - 1
        while self.taken <= last:
            self.hand(self.taken)
            self.handed[self.taken].wait_recv()
            self.taken += 1

    def left(self):
        for copy in self.direct + self.handed:
            copy.wait_send()


def layer_kernel(n, n_mp, bounds, names, *refs):
    R = types.SimpleNamespace(**dict(zip(names, refs)))
    at = Place(n, n_mp)
    s, m, hi, lo, y, core = at.s, at.m, at.hi, at.lo, at.y, at.core
    per, wide, lines = at.per, at.wide, at.lines
    rows, width = R.out.shape[0] // HALVES, R.out.shape[1]
    bf16, f32 = jnp.bfloat16, jnp.float32
    sends = []

    def part(h):
        return slice(h * rows, (h + 1) * rows)

    loads = {}
    slots = iter(range(R.w_sems.shape[0]))

    def load(name, src, dst):
        loads[name] = pltpu.make_async_copy(src, dst, R.w_sems.at[next(slots)])
        loads[name].start()

    load("tokens", R.tokens_hbm, R.tokens)
    load("gain_attn", R.gain_attn_hbm, R.gain_attn)
    load("bias", R.bias_hbm, R.bias)
    load("w_query", R.w_query_hbm, R.w_query)
    load("keys", R.keys_hbm, R.keys)
    load("values", R.values_hbm, R.values)
    load("gain_ffn", R.gain_ffn_hbm, R.gain_ffn)
    span = D // KV_HEADS
    for g in range(KV_HEADS):
        load(f"w_out{g}", R.w_out_hbm.at[:, pl.ds(g * span, span)], R.w_out.at[g])
    load("gate", R.gate_hbm, R.gate_w)
    load("up", R.up_hbm, R.up_w)
    load("down", R.down_hbm, R.down_w)
    everyone_here = greet(at)

    loads["tokens"].wait()
    hidden_in = R.tokens[...].astype(f32)
    mean_sq = jnp.sum(hidden_in * hidden_in, axis=1, keepdims=True) / D
    loads["gain_attn"].wait()
    normed = (hidden_in * lax.rsqrt(mean_sq + eps) * R.gain_attn[...]).astype(bf16)
    loads["bias"].wait()
    loads["w_query"].wait()
    queries = (times_transposed(normed, R.w_query[...]) + R.bias[...]).astype(bf16)
    for h in range(HALVES):
        R.qbuf[h, s] = queries[part(h)]
    everyone_here()
    asked = [Gather(at, R.qbuf.at[h], R.q_sems.at[h]) for h in range(HALVES)]
    for flow in asked:
        flow.start()
    for k in range(n):

        @pl.when(s == k)
        def _():
            R.own_tokens[...] = R.tokens[:, k * width : (k + 1) * width].astype(f32)

    def attend(h, j):
        g = at.group(j)
        q = jnp.concatenate([R.qbuf[h, g * wide + i] for i in range(wide)], axis=1)
        stacked = jnp.concatenate([q[:, i * HEAD : (i + 1) * HEAD] for i in range(GROUP)], axis=0)
        scores = times_transposed(stacked, R.keys[g])
        highest = jnp.max(scores, axis=1, keepdims=True)
        probs = jnp.exp2((scores - highest) * EXP2_SCALE)
        sums = jnp.sum(probs, axis=1, keepdims=True)
        weighted = jnp.dot(probs.astype(bf16), R.values[g], preferred_element_type=f32)
        side = jnp.concatenate([weighted[part(i)] for i in range(GROUP)], axis=1).astype(bf16)
        for i in range(wide):
            R.part_out[h, g * wide + i] = side[:, i * width : (i + 1) * width]
        R.stat_out[h, g] = jnp.zeros((2 * SUM_ROW, rows), f32)
        for i in range(GROUP):
            R.stat_out[h, g, i : i + 1, :] = column_to_row(highest[part(i)] * EXP2_SCALE)
            R.stat_out[h, g, i + SUM_ROW : i + SUM_ROW + 1, :] = column_to_row(sums[part(i)])
        for i in range(wide):
            to = g * wide + lax.rem(s + i, wide)
            if i == 0 and j == 0:
                R.part_in[h, s] = R.part_out[h, s]
                R.stat_in[h, s] = R.stat_out[h, g]
                continue
            for src, dst, k in (
                (R.part_out.at[h, to], R.part_in.at[h, s], 0),
                (R.stat_out.at[h, g], R.stat_in.at[h, s], 1),
            ):
                copy = push(
                    src, dst, R.m_send.at[h, k, j * wide + i], R.m_recv.at[h, k, s], (to, m)
                )
                copy.start()
                sends.append(copy)

    def merge(h):
        for d in range(1, n):
            source = lax.rem(s + d, n)
            for src, dst, k in (
                (R.part_out.at[h, 0], R.part_in.at[h, source], 0),
                (R.stat_out.at[h, 0], R.stat_in.at[h, source], 1),
            ):
                sem = R.m_recv.at[h, k, source]
                push(src, dst, sem, sem, (source, m)).wait_recv()
        maxima, sums = R.stat_in[h, :, :SUM_ROW, :], R.stat_in[h, :, SUM_ROW:, :]
        rescale = jnp.exp2(maxima - jnp.max(maxima, axis=0, keepdims=True))
        total = jnp.sum(sums * rescale, axis=0)
        row = lax.broadcasted_iota(jnp.int32, (SUM_ROW, rows), 0)
        inverse = 1.0 / jnp.where(row < GROUP, total, 1.0)
        shape = (2 * SUM_ROW, width)
        column = s * width + lax.broadcasted_iota(jnp.int32, shape, 1)
        head = lax.div(column, HEAD) - s // wide * GROUP
        index = lax.rem(lax.broadcasted_iota(jnp.int32, shape, 0), SUM_ROW)
        pick = jnp.where(head == index, 1.0, 0.0).astype(bf16)
        result = jnp.zeros((rows, width), f32)
        for j in range(n):
            exact = rescale[j] * inverse
            coarse = exact.astype(bf16).astype(f32)
            pair = jnp.concatenate([coarse, exact - coarse], axis=0).astype(bf16)
            factor = lax.dot_general(
                pair, pick, (((0,), (0,)), ((), ())), preferred_element_type=f32
            )
            result = result + R.part_in[h, j].astype(f32) * factor
        R.att[h, s] = result.astype(bf16)
        R.attended[part(h), :] = result.astype(bf16)

    def project(h, flow):
        total = R.own_tokens[part(h), :]
        for j in range(KV_HEADS):
            flow.take(j)
            g = at.group(j)
            block = jnp.concatenate([R.att[h, g * wide + i] for i in range(wide)], axis=1)
            total = total + times_transposed(block, R.w_out[g])
        R.residual[part(h), :] = total
        R.lined[h, hi] = (total * R.gain_ffn[...]).astype(bf16)
        R.squares[h, s] = column_to_row(jnp.sum(total * total, axis=1, keepdims=True))
        for d in range(1, lines):
            copy = push(
                R.lined.at[h, hi], R.lined.at[h, hi], R.l_sems.at[h, 0, d], R.l_sems.at[h, 1, d],
                (at.ahead(d) * 2 + lo, m),
            )
            copy.start()
            lined[h].append(copy)
        for d in range(1, n):
            copy = push(
                R.squares.at[h, s], R.squares.at[h, s], R.sq_sems.at[h, 0, d],
                R.sq_sems.at[h, 1, d], (lax.rem(s + d, n), m),
            )
            copy.start()
            squared[h].append(copy)

    lined = [[] for _ in range(HALVES)]
    squared = [[] for _ in range(HALVES)]
    relayed = []

    def relay(h):
        for d in range(lines):
            if d:
                lined[h][d - 1].wait_recv()
            line = at.behind(d)
            source = line * 2 + lo
            to_m, k = source // per, lax.rem(source, per)
            for b in range(2):
                copy = push(
                    R.lined.at[h, line], R.blocks.at[h, m, k], R.r_send.at[h, b, d],
                    R.r_recv.at[h, m, k], at.near(b, to_m),
                )
                if b:
                    copy.start()
                    sends.append(copy)
                    continue
                here = to_m == m

                @pl.when(here)
                def _():
                    R.blocks[h, m, k] = R.lined[h, line]

                @pl.when(jnp.logical_not(here))
                def _():
                    copy.start()

                relayed.append((here, copy))

    order = (1 - core, 3 - core, core, 2 + core)

    def collect(h):
        for i in range(n_mp):
            source = lax.rem(m + i, n_mp)
            for k in range(per):
                if i == 0 and k % 2 == 0:
                    continue
                at_k = k // 2 * 2 + lax.rem(lo + k, 2)
                sem = R.r_recv.at[h, source, at_k]
                push(
                    R.lined.at[h, 0], R.blocks.at[h, source, at_k], sem, sem,
                    at.near(k % 2, source),
                ).wait_recv()
        for p, t in enumerate(order):
            R.features[h, p * rows : (p + 1) * rows, :] = jnp.concatenate(
                [R.blocks[h, t, j] for j in range(per)], axis=1
            )

    def inverse_of(h):
        for copy in squared[h]:
            copy.wait_recv()
        return row_to_column(lax.rsqrt(jnp.sum(R.squares[h], axis=0) / D + eps))

    chunks = []
    for c, (h, first, last) in enumerate(bounds):
        kept, s1_out, s1_in, s2_out, s2_in, act = (
            getattr(R, f"{name}{c}") for name in ("kept", "s1_out", "s1_in", "s2_out", "s2_in", "act")
        )
        sem = lambda k, c=c: R.c_sems.at[c, k]
        chunks.append(
            dict(
                half=h, first=first, last=last, kept=kept, s1_out=s1_out, s1_in=s1_in,
                s2_out=s2_out, s2_in=s2_in, act=act,
                s1=push(s1_out, s1_in, sem(0), sem(1), at.sibling),
                s2=push(s2_out, s2_in, sem(2), sem(3), at.across),
                near=push(act.at[m], act.at[m], sem(4), sem(5), at.sibling),
                far=push(act.at[m], act.at[m], sem(6), sem(7), at.across),
                relay=push(
                    act.at[at.across[1]], act.at[at.across[1]], sem(8), sem(9), at.sibling
                ),
            )
        )
    halves = [[ch for ch in chunks if ch["half"] == h] for h in range(HALVES)]

    def multiply(ch):
        for g, weight in enumerate((R.gate_w, R.up_w)):
            product = times_transposed(R.features[ch["half"]], weight[ch["first"] : ch["last"], :])
            for p in range(2):
                ch["s1_out"][g, p] = product[p * rows : (p + 1) * rows].astype(bf16)
                ch["kept"][g, p] = product[(p + 2) * rows : (p + 3) * rows]
        ch["s1"].start()

    def pair_sum(ch):
        ch["s1"].wait_recv()
        for g in range(2):
            ch["s2_out"][g] = (
                ch["kept"][g, 1 - y] + ch["s1_in"][g, 1 - y].astype(f32)
            ).astype(bf16)
        ch["s2"].start()

    def activate(ch, inverse):
        ch["s2"].wait_recv()
        gate, up = [
            (ch["kept"][g, y] + ch["s1_in"][g, y].astype(f32) + ch["s2_in"][g].astype(f32))
            * inverse
            for g in range(2)
        ]
        ch["act"][m] = (gate / (1.0 + jnp.exp(-gate)) * up).astype(bf16)
        ch["far"].start()
        ch["near"].start()

    def finish(h):
        own = halves[h]
        for c, ch in enumerate(own):
            ch["far"].wait_recv()
            ch["relay"].start()
            ch["near"].wait_recv()
            ch["relay"].wait_recv()
            act = ch["act"][...].reshape(n_mp * rows, ch["last"] - ch["first"])
            product = jnp.dot(
                act, R.down_w[ch["first"] : ch["last"], :], preferred_element_type=f32
            )
            total = product if c == 0 else R.acc[...] + product
            if c < len(own) - 1:
                R.acc[...] = total
        for t in range(n_mp):
            for k in range(per):
                R.down_out[h, t, k % 2, k // 2] = total[
                    t * rows : (t + 1) * rows, k * width : (k + 1) * width
                ].astype(bf16)
        for i in range(n_mp):
            for b in range(2):
                if i == 0 and b == 0:
                    R.home_in[h, lo, m] = R.down_out[h, m, lo]
                    continue
                to_m, to_lo = lax.rem(m + i, n_mp), lax.rem(lo + b, 2)
                copy = push(
                    R.down_out.at[h, to_m, to_lo], R.home_in.at[h, lo, m],
                    R.h_sems.at[h, 0, i * 2 + b], R.h_sems.at[h, 1, i * 2 + b], at.near(b, to_m),
                )
                copy.start()
                homed[h].append(copy)

    homed = [[] for _ in range(HALVES)]
    lastly = []

    def send_home(h):
        arrivals = iter(homed[h])
        for i in range(n_mp):
            source = lax.rem(m + n_mp - i, n_mp)
            for b in range(2):
                if i or b:
                    next(arrivals).wait_recv()
            for k in range(per // 2):
                line = source * (per // 2) + k
                total = R.home_in[h, 0, source, k].astype(f32) + R.home_in[h, 1, source, k].astype(f32)
                R.home_out[h, line] = total.astype(bf16)
                here = line == hi
                copy = push(
                    R.home_out.at[h, line], R.terms.at[h, hi], R.t_send.at[h, line],
                    R.t_recv.at[h, hi], (line * 2 + lo, m),
                )

                @pl.when(here)
                def _():
                    R.terms[h, hi] = R.home_out[h, line]

                @pl.when(jnp.logical_not(here))
                def _():
                    copy.start()

                lastly.append((here, copy))

    def conclude(h):
        for d in range(1, lines):
            line = at.behind(d)
            sem = R.t_recv.at[h, line]
            push(
                R.home_out.at[h, 0], R.terms.at[h, line], sem, sem, (line * 2 + lo, m)
            ).wait_recv()
        result = R.residual[part(h), :]
        for i in range(lines):
            result = result + R.terms[h, i].astype(f32)
        R.out[part(h), :] = result.astype(bf16)

    loads["keys"].wait()
    loads["values"].wait()
    for h in range(HALVES):
        for j in range(KV_HEADS):
            asked[h].take(j)
            if h + 1 < HALVES and lines == KV_HEADS:
                asked[h + 1].hand(j)
            attend(h, j)
    for g in range(KV_HEADS):
        loads[f"w_out{g}"].wait()
    loads["gain_ffn"].wait()
    answered = [Gather(at, R.att.at[h], R.a_sems.at[h]) for h in range(HALVES)]
    for h in range(HALVES):
        merge(h)
        answered[h].start()
    for h in range(HALVES):
        project(h, answered[h])
    relay(0)
    collect_next = 0
    loads["gate"].wait()
    loads["up"].wait()
    for h in range(1, HALVES):
        relay(h)
    collect(0)
    for c, ch in enumerate(halves[0]):
        multiply(ch)
        if c >= 1:
            pair_sum(halves[0][c - 1])
    pair_sum(halves[0][-1])
    inverse = [None] * HALVES
    inverse[0] = inverse_of(0)
    for h in range(1, HALVES):
        collect(h)
        for ch in halves[h]:
            multiply(ch)
        for ch in halves[h - 1]:
            activate(ch, inverse[h - 1])
        for ch in halves[h]:
            pair_sum(ch)
        inverse[h] = inverse_of(h)
        if h == 1:
            loads["down"].wait()
        else:
            send_home(h - 2)
        finish(h - 1)
    for ch in halves[-1]:
        activate(ch, inverse[-1])
    send_home(HALVES - 2)
    finish(HALVES - 1)
    send_home(HALVES - 1)
    for h in range(HALVES):
        conclude(h)

    for flow in asked + answered:
        flow.left()
    for copies in lined + squared + homed:
        sends.extend(copies)
    for copy in sends:
        copy.wait_send()
    for here, copy in relayed + lastly:

        @pl.when(jnp.logical_not(here))
        def _():
            copy.wait_send()

    for ch in chunks:
        for name in ("s1", "s2", "near", "far", "relay"):
            ch[name].wait_send()


def layer(n, n_mp, *arrays):
    tokens, w_query, keys, w_gate, w_down = (arrays[i] for i in (0, 2, 4, 8, 10))
    rows, width = tokens.shape[0], w_query.shape[0]
    hidden, quarter = w_gate.shape
    lines, per = n // 2, n // n_mp
    step = max(128, -(-hidden // CHUNKS // 128) * 128)
    bounds = [
        (h, first, min(first + step, hidden))
        for h in range(HALVES)
        for first in range(0, hidden, step)
    ]
    part = rows // HALVES
    bf16, f32, dma = jnp.bfloat16, jnp.float32, pltpu.SemaphoreType.DMA
    scratch = dict(
        tokens=VMEM(tokens.shape, bf16),
        gain_attn=VMEM((1, D), f32),
        bias=VMEM((1, width), f32),
        gain_ffn=VMEM((1, width), f32),
        w_query=VMEM(w_query.shape, bf16),
        keys=VMEM(keys.shape, bf16),
        values=VMEM(keys.shape, bf16),
        w_out=VMEM((KV_HEADS, width, D // KV_HEADS), bf16),
        gate_w=VMEM(w_gate.shape, bf16),
        up_w=VMEM(w_gate.shape, bf16),
        down_w=VMEM(w_down.shape, bf16),
        own_tokens=VMEM((rows, width), f32),
        residual=VMEM((rows, width), f32),
        qbuf=VMEM((HALVES, n, part, width), bf16),
        part_out=VMEM((HALVES, n, part, width), bf16),
        part_in=VMEM((HALVES, n, part, width), bf16),
        stat_out=VMEM((HALVES, KV_HEADS, 2 * SUM_ROW, part), f32),
        stat_in=VMEM((HALVES, n, 2 * SUM_ROW, part), f32),
        att=VMEM((HALVES, n, part, width), bf16),
        lined=VMEM((HALVES, lines, part, width), bf16),
        squares=VMEM((HALVES, n, 1, part), f32),
        blocks=VMEM((HALVES, n_mp, per, part, width), bf16),
        features=VMEM((HALVES, n_mp * part, quarter), bf16),
        acc=VMEM((n_mp * part, w_down.shape[1]), f32),
        down_out=VMEM((HALVES, n_mp, 2, per // 2, part, width), bf16),
        home_in=VMEM((HALVES, 2, n_mp, per // 2, part, width), bf16),
        home_out=VMEM((HALVES, lines, part, width), bf16),
        terms=VMEM((HALVES, lines, part, width), bf16),
        w_sems=dma((10 + KV_HEADS,)),
        q_sems=dma((HALVES, 4, lines)),
        a_sems=dma((HALVES, 4, lines)),
        m_send=dma((HALVES, 2, n)),
        m_recv=dma((HALVES, 2, n)),
        l_sems=dma((HALVES, 2, lines)),
        sq_sems=dma((HALVES, 2, n)),
        r_send=dma((HALVES, 2, lines)),
        r_recv=dma((HALVES, n_mp, per)),
        h_sems=dma((HALVES, 2, 2 * n_mp)),
        t_send=dma((HALVES, lines)),
        t_recv=dma((HALVES, lines)),
        c_sems=dma((len(bounds), 10)),
    )
    for c, (_, first, last) in enumerate(bounds):
        span = last - first
        scratch[f"kept{c}"] = VMEM((2, 2, part, span), f32)
        scratch[f"s1_out{c}"] = VMEM((2, 2, part, span), bf16)
        scratch[f"s1_in{c}"] = VMEM((2, 2, part, span), bf16)
        scratch[f"s2_out{c}"] = VMEM((2, part, span), bf16)
        scratch[f"s2_in{c}"] = VMEM((2, part, span), bf16)
        scratch[f"act{c}"] = VMEM((n_mp, part, span), bf16)
    names = ARGS + OUTS + tuple(scratch)
    block = jax.ShapeDtypeStruct((rows, width), bf16)
    vmem, anywhere = pl.BlockSpec(memory_space=VMEM), pl.BlockSpec(memory_space=pl.ANY)
    return pl.pallas_call(
        functools.partial(layer_kernel, n, n_mp, bounds, names),
        out_shape=(block, block),
        in_specs=[anywhere] * len(ARGS),
        out_specs=(vmem, vmem),
        scratch_shapes=list(scratch.values()),
        compiler_params=pltpu.CompilerParams(
            collective_id=1, has_side_effects=True, vmem_limit_bytes=60 * 2**20
        ),
        name="layer",
    )(*arrays)


def body(
    n_seq,
    n_mp,
    tokens,
    gain_attn,
    w_query,
    query_bias,
    cache_keys,
    cache_values,
    w_out,
    gain_ffn,
    w_gate,
    w_up,
    w_down,
):
    return layer(
        n_seq,
        n_mp,
        tokens,
        gain_attn[None, :],
        w_query.T,
        query_bias[None, :],
        cache_keys,
        cache_values,
        w_out.T,
        gain_ffn[None, :],
        w_gate.T,
        w_up.T,
        w_down,
    )


def solution(mesh):
    placed = (
        P("mp", None),
        P(),
        P(None, "seq"),
        P("seq"),
        P(None, "seq", None),
        P(None, "seq", None),
        P(None, "seq"),
        P("seq"),
        P("mp", "seq"),
        P("mp", "seq"),
        P("seq", "mp"),
    )
    return jax.shard_map(
        functools.partial(body, mesh.shape["seq"], mesh.shape["mp"]),
        mesh=mesh,
        in_specs=placed,
        out_specs=(P("mp", "seq"), P("mp", "seq")),
        check_vma=False,
    )
```

time: 131 us -> 107 us (0.82); the launches traced: 129 us -> 106 us
  Pallas kernels: 120 us -> 101 us
  matrix products: 2.71 us -> 0 us
  other arithmetic: 2.45 us -> 0 us
  local copies, waits for them, and re-layouts: 2.89 us -> 4.27 us
    pallas_call x7 -> x1, Pallas kernels: 120 us -> 101 us  [layer(): pl.pallas_call(functools.partial(layer_kernel, n, n_mp, bounds, names), o...]
    dot_general x1 -> x0, matrix products: 2.71 us -> none  [body(): jnp.dot(normed, w_query, preferred_element_type=jnp.float32) + query_bias]
    reduce_sum x1 -> x0, other arithmetic: 1.36 us -> none  [body(): mean_sq = jnp.mean(hidden_in * hidden_in, axis=1, keepdims=True)]
    broadcast_in_dim x0 -> x1, local copies, waits for them, and re-layouts: none -> 1.33 us  [body(): gain_attn[None, :]]
    unnamed x3 -> x2, local copies, waits for them, and re-layouts: 2.14 us -> 2.95 us
where the time goes in v1:
time: 107 us; the launch traced here: 106 us
  Pallas kernels  101 us (94%)
  local copies, waits for them, and re-layouts  4.27 us (4%)
    pallas_call x1, Pallas kernels, layer(): pl.pallas_call(functools.partial(layer_kernel, n, n_mp, bounds, names), o...  101 us
    unnamed x2, local copies, waits for them, and re-layouts  2.95 us

profile of v1, /device:TPU:5, one launch (start us, length us, event | category | flops | bytes accessed | tf_op | source)
XLA Modules:
  0.0 106.3 jit_solution(12124510637940551250)
XLA Ops:
  0.6 1.3 %broadcast_in_dim.9.refs_1_ = f32[1,3584]{1,0:T(1,128)} reshape(f32[3584]{0:T(1024)} %param.12) | data formatting | bytes 28672 | tf_op jit(solution)/shard_map/broadcast_in_dim | solution.py:625
  2.0 101.4 %layer.1 = (bf16[64,448]{1,0:T(8,128)(2,1)}, bf16[64,448]{1,0:T(8,128)(2,1)}) custom-call(bf16[64,3584]{1,0:T(8,128)(2,1)} %refs_0_.1, f32[1,3584]{1,0:T(1,128)} %broadcast_in_dim.9.refs_1_, bf16[448,3584]{1,0:T(8,128)(2,1)} %bitcast.8, f32[1,448]{1,0:T(1,128)} %bitcast.10, bf16[4,1024,128]{2,1,0:T(8,128)(2,1)} %refs_4_.1, bf16[4,1024,128]{2,1,0:T(8,128)(2,1)} %refs_5_.1, ...), custom_call_target="tpu_custom_call" | custom-call | tf_op jit(solution)/shard_map/layer/pallas_call | solution.py:593
  103.3 1.5 %copy.15 = bf16[64,448]{1,0:T(8,128)(2,1)} copy(bf16[64,448]{1,0:T(8,128)(2,1)} %get-tuple-element.4) | data formatting | bytes 114688
  104.8 1.5 %copy.16 = bf16[64,448]{1,0:T(8,128)(2,1)} copy(bf16[64,448]{1,0:T(8,128)(2,1)} %get-tuple-element.5) | data formatting | bytes 114688

commit v2 on v1

v2 whole, which is shorter than its diff:
```python
import functools
import math
import types

import jax
import jax.numpy as jnp
from jax import lax
from jax.experimental import pallas as pl
from jax.experimental.pallas import tpu as pltpu
from jax.sharding import PartitionSpec as P

D = 3584
HEADS = 28
KV_HEADS = 4
HEAD = 128
GROUP = HEADS // KV_HEADS
SUM_ROW = 8
CUTS = ((0.25, 0.6), (0.4, 0.75))
HALVES = 2
LAG = 2

eps = 1e-06
EXP2_SCALE = HEAD ** (-0.5) * math.log2(math.e)
MESH = pl.DeviceIdType.MESH
VMEM = pltpu.VMEM
ARGS = (
    "tokens_hbm", "gain_attn_hbm", "w_query_hbm", "bias_hbm", "keys_hbm", "values_hbm",
    "w_out_hbm", "gain_ffn_hbm", "gate_hbm", "up_hbm", "down_hbm",
)
OUTS = ("attended", "out")


def push(src, dst, send, recv, to):
    return pltpu.make_async_remote_copy(
        src_ref=src,
        dst_ref=dst,
        send_sem=send,
        recv_sem=recv,
        device_id=to,
        device_id_type=MESH,
    )


def times_transposed(a, b):
    return lax.dot_general(a, b, (((1,), (1,)), ((), ())), preferred_element_type=jnp.float32)


def row_to_column(row):
    k = row.shape[1]
    across = lax.broadcasted_iota(jnp.int32, (k, k), 1)
    down = lax.broadcasted_iota(jnp.int32, (k, k), 0)
    return jnp.sum(jnp.where(across == down, row, 0.0), axis=1, keepdims=True)


def column_to_row(column):
    k = column.shape[0]
    across = lax.broadcasted_iota(jnp.int32, (k, k), 1)
    down = lax.broadcasted_iota(jnp.int32, (k, k), 0)
    return jnp.sum(jnp.where(across == down, column, 0.0), axis=0, keepdims=True)


class Place:
    def __init__(self, n, n_mp):
        self.n, self.n_mp = n, n_mp
        self.lines, self.per, self.wide = n // 2, n // n_mp, n // KV_HEADS
        self.s, self.m = lax.axis_index("seq"), lax.axis_index("mp")
        self.hi, self.lo = self.s // 2, lax.rem(self.s, 2)
        self.y, self.core = self.m // 2, lax.rem(self.m, 2)
        self.partner = (self.hi * 2 + 1 - self.lo, self.m)
        self.sibling = (self.s, self.y * 2 + (1 - self.core))
        self.across = (self.s, (1 - self.y) * 2 + self.core)

    def ahead(self, d):
        return lax.rem(self.hi + d, self.lines)

    def behind(self, d):
        return lax.rem(self.hi + self.lines - d, self.lines)

    def near(self, b, m):
        return (self.hi * 2 + lax.rem(self.lo + b, 2), m)

    def group(self, j):
        return lax.rem(self.s // self.wide + KV_HEADS - j, KV_HEADS)


def greet(at):
    barrier = pltpu.get_barrier_semaphore()
    peers = [(lax.rem(at.s + d, at.n), at.m) for d in range(1, at.n)]
    peers += [
        at.near(b, lax.rem(at.m + i, at.n_mp)) for i in range(1, at.n_mp) for b in range(2)
    ]
    for peer in peers:
        pl.semaphore_signal(barrier, inc=1, device_id=peer, device_id_type=MESH)
    return lambda: pl.semaphore_wait(barrier, len(peers))


class Gather:
    def __init__(self, at, buf, sems, sent):
        self.at, self.buf, self.sems, self.sent = at, buf, sems, sent
        self.direct = [
            push(
                buf.at[at.s], buf.at[at.s], sent.sem, sems.at[0, d],
                (at.ahead(d) * 2 + at.lo, at.m),
            )
            for d in range(1, at.lines)
        ]
        self.handed, self.taken = [], 0

    def start(self):
        for copy in self.direct:
            copy.start()
            self.sent.count += 1
        self.hand(0)

    def hand(self, d):
        at = self.at
        if d < len(self.handed):
            return
        if d:
            self.direct[d - 1].wait_recv()
        block = self.buf.at[at.behind(d) * 2 + at.lo]
        copy = push(block, block, self.sent.sem, self.sems.at[1, d], at.partner)
        copy.start()
        self.handed.append(copy)
        self.sent.count += 1

    def hand_all(self):
        for d in range(self.at.lines):
            self.hand(d)

    def take(self, j):
        last = j if self.at.lines == KV_HEADS else self.at.lines - 1
        while self.taken <= last:
            self.hand(self.taken)
            self.handed[self.taken].wait_recv()
            self.taken += 1


class Sent:
    def __init__(self, sem, sized, to):
        self.sem, self.sized, self.to, self.count = sem, sized, to, 0

    def start(self, copy, blocks=1):
        copy.start()
        self.count += blocks

    def wait(self):
        of = self.sized.at[pl.ds(0, self.count)]
        push(of, of, self.sem, self.sem, self.to).wait_send()


def arrival(sized, count, sem, source):
    of = sized.at[pl.ds(0, count)]
    return push(of, of, sem, sem, source)


def layer_kernel(n, n_mp, bounds, names, *refs):
    R = types.SimpleNamespace(**dict(zip(names, refs)))
    at = Place(n, n_mp)
    s, m, hi, lo, y, core = at.s, at.m, at.hi, at.lo, at.y, at.core
    per, wide, lines = at.per, at.wide, at.lines
    rows, width = R.out.shape[0] // HALVES, R.out.shape[1]
    bf16, f32 = jnp.bfloat16, jnp.float32
    sent = Sent(R.s_sems.at[0], R.sized, at.partner)
    sent_stats = Sent(R.s_sems.at[1], R.sized_stats, at.partner)
    sent_squares = Sent(R.s_sems.at[2], R.sized_squares, at.partner)

    def part(h):
        return slice(h * rows, (h + 1) * rows)

    loads = {}
    slots = iter(range(R.w_sems.shape[0]))

    def load(name, src, dst):
        loads[name] = pltpu.make_async_copy(src, dst, R.w_sems.at[next(slots)])
        loads[name].start()

    load("tokens", R.tokens_hbm, R.tokens)
    load("gain_attn", R.gain_attn_hbm, R.gain_attn)
    load("bias", R.bias_hbm, R.bias)
    load("w_query", R.w_query_hbm, R.w_query)
    load("gain_ffn", R.gain_ffn_hbm, R.gain_ffn)
    everyone_here = greet(at)

    loads["tokens"].wait()
    hidden_in = R.tokens[...].astype(f32)
    mean_sq = jnp.sum(hidden_in * hidden_in, axis=1, keepdims=True) / D
    loads["gain_attn"].wait()
    normed = (hidden_in * lax.rsqrt(mean_sq + eps) * R.gain_attn[...].reshape(1, D)).astype(bf16)
    loads["bias"].wait()
    loads["w_query"].wait()
    load("keys", R.keys_hbm, R.keys)
    load("values", R.values_hbm, R.values)
    queries = (times_transposed(normed, R.w_query[...]) + R.bias[...]).astype(bf16)
    for h in range(HALVES):
        R.qbuf[h, s] = queries[part(h)]
    everyone_here()
    asked = [Gather(at, R.qbuf.at[h], R.q_sems.at[h], sent) for h in range(HALVES)]
    for flow in asked:
        flow.start()
    span = D // KV_HEADS
    for g in range(KV_HEADS):
        load(f"w_out{g}", R.w_out_hbm.at[:, pl.ds(g * span, span)], R.w_out.at[g])
    load("gate", R.gate_hbm, R.gate_w)
    load("up", R.up_hbm, R.up_w)
    load("down", R.down_hbm, R.down_w)
    for k in range(n):

        @pl.when(s == k)
        def _():
            R.own_tokens[...] = R.tokens[:, k * width : (k + 1) * width].astype(f32)

    def attend(h, j):
        g = at.group(j)
        q = jnp.concatenate([R.qbuf[h, g * wide + i] for i in range(wide)], axis=1)
        stacked = jnp.concatenate([q[:, i * HEAD : (i + 1) * HEAD] for i in range(GROUP)], axis=0)
        scores = times_transposed(stacked, R.keys[g])
        highest = jnp.max(scores, axis=1, keepdims=True)
        probs = jnp.exp2((scores - highest) * EXP2_SCALE)
        sums = jnp.sum(probs, axis=1, keepdims=True)
        weighted = jnp.dot(probs.astype(bf16), R.values[g], preferred_element_type=f32)
        side = jnp.concatenate([weighted[part(i)] for i in range(GROUP)], axis=1).astype(bf16)
        for i in range(wide):
            R.part_out[h, j, i % 2, i // 2] = side[:, i * width : (i + 1) * width]
        R.stat_out[h, j] = jnp.zeros((2 * SUM_ROW, rows), f32)
        for i in range(GROUP):
            R.stat_out[h, j, i : i + 1, :] = column_to_row(highest[part(i)] * EXP2_SCALE)
            R.stat_out[h, j, i + SUM_ROW : i + SUM_ROW + 1, :] = column_to_row(sums[part(i)])
        for src, dst, k, record, blocks in (
            (R.part_out.at[h, j, 1 - lo], R.pair_in.at[h, j], 0, sent, wide // 2),
            (R.stat_out.at[h, j], R.pair_stat.at[h, j], 1, sent_stats, 1),
        ):
            copy = push(src, dst, record.sem, R.p_sems.at[h, k, j], at.partner)
            record.start(copy, blocks)
            paired[h, j].append(copy)

    paired = {(h, j): [] for h in range(HALVES) for j in range(KV_HEADS)}
    index = lax.rem(lax.broadcasted_iota(jnp.int32, (2 * SUM_ROW, width), 0), SUM_ROW)
    picks = []
    for k in range(wide // 2):
        first = (k * 2 + lo) * width
        column = first + lax.broadcasted_iota(jnp.int32, (2 * SUM_ROW, width), 1)
        picks.append(jnp.where(lax.div(column, HEAD) == index, 1.0, 0.0).astype(bf16))

    def spread(factor, pick):
        coarse = factor.astype(bf16).astype(f32)
        pair = jnp.concatenate([coarse, factor - coarse], axis=0).astype(bf16)
        return lax.dot_general(pair, pick, (((0,), (0,)), ((), ())), preferred_element_type=f32)

    def join(h, j):
        for copy in paired[h, j]:
            copy.wait_recv()
        mine, other = R.stat_out[h, j], R.pair_stat[h, j]
        top = jnp.maximum(mine[:SUM_ROW], other[:SUM_ROW])
        scale, scale_other = jnp.exp2(mine[:SUM_ROW] - top), jnp.exp2(other[:SUM_ROW] - top)
        R.line_stat[h, j, :SUM_ROW, :] = top
        R.line_stat[h, j, SUM_ROW:, :] = mine[SUM_ROW:] * scale + other[SUM_ROW:] * scale_other
        g = at.group(j)
        for k in range(wide // 2):
            total = R.part_out[h, j, lo, k].astype(f32) * spread(scale, picks[k]) + R.pair_in[
                h, j, k
            ].astype(f32) * spread(scale_other, picks[k])
            R.line_out[h, j, k] = total.astype(bf16)
            line = g * (wide // 2) + k
            if wide // 2 == 1 and j == 0:
                R.part_in[h, hi] = R.line_out[h, j, k]
                R.stat_in[h, hi] = R.line_stat[h, j]
                continue
            for src, dst, kind, record in (
                (R.line_out.at[h, j, k], R.part_in.at[h, hi], 0, sent),
                (R.line_stat.at[h, j], R.stat_in.at[h, hi], 1, sent_stats),
            ):
                copy = push(src, dst, record.sem, R.m_recv.at[h, kind], (line * 2 + lo, m))
                if j:
                    record.start(copy)
                    continue

                @pl.when(line != hi)
                def _():
                    copy.start()

                record.count += int(k > 0)
            if j == 0:

                @pl.when(line == hi)
                def _():
                    R.part_in[h, hi] = R.line_out[h, j, k]
                    R.stat_in[h, hi] = R.line_stat[h, j]

    def merge(h):
        arrival(R.sized, lines - 1, R.m_recv.at[h, 0], at.partner).wait_recv()
        arrival(R.sized_stats, lines - 1, R.m_recv.at[h, 1], at.partner).wait_recv()
        maxima, sums = R.stat_in[h, :, :SUM_ROW, :], R.stat_in[h, :, SUM_ROW:, :]
        rescale = jnp.exp2(maxima - jnp.max(maxima, axis=0, keepdims=True))
        total = jnp.sum(sums * rescale, axis=0)
        row = lax.broadcasted_iota(jnp.int32, (SUM_ROW, rows), 0)
        inverse = 1.0 / jnp.where(row < GROUP, total, 1.0)
        column = lax.rem(s, wide) * width + lax.broadcasted_iota(
            jnp.int32, (2 * SUM_ROW, width), 1
        )
        pick = jnp.where(lax.div(column, HEAD) == index, 1.0, 0.0).astype(bf16)
        result = jnp.zeros((rows, width), f32)
        for i in range(lines):
            result = result + R.part_in[h, i].astype(f32) * spread(rescale[i] * inverse, pick)
        R.att[h, s] = result.astype(bf16)
        copy = pltpu.make_async_copy(R.att.at[h, s], R.attended.at[pl.ds(h * rows, rows)], R.o_sems.at[0, h])
        copy.start()
        written.append(copy)

    written = []

    def project(h, flow):
        total = R.own_tokens[part(h), :]
        for j in range(KV_HEADS):
            flow.take(j)
            g = at.group(j)
            block = jnp.concatenate([R.att[h, g * wide + i] for i in range(wide)], axis=1)
            total = total + times_transposed(block, R.w_out[g])
        R.residual[part(h), :] = total
        R.lined[h, hi] = (total * R.gain_ffn[...]).astype(bf16)
        R.squares[h, s] = column_to_row(jnp.sum(total * total, axis=1, keepdims=True))
        for d in range(1, lines):
            copy = push(
                R.lined.at[h, hi], R.lined.at[h, hi], sent.sem, R.l_sems.at[h, d],
                (at.ahead(d) * 2 + lo, m),
            )
            sent.start(copy)
            lined[h].append(copy)
        relay(h, range(1))
        for d in range(1, n):
            copy = push(
                R.squares.at[h, s], R.squares.at[h, s], sent_squares.sem, R.sq_sems.at[h],
                (lax.rem(s + d, n), m),
            )
            sent_squares.start(copy)

    lined = [[] for _ in range(HALVES)]

    def relay(h, steps):
        for d in steps:
            if d:
                lined[h][d - 1].wait_recv()
            line = at.behind(d)
            source = line * 2 + lo
            to_m, k = source // per, lax.rem(source, per)
            for b in range(2):
                copy = push(
                    R.lined.at[h, line], R.blocks.at[h, m, k], sent.sem, R.r_recv.at[h],
                    at.near(b, to_m),
                )
                if b:
                    sent.start(copy)
                    continue

                @pl.when(to_m == m)
                def _():
                    R.blocks[h, m, k] = R.lined[h, line]

                @pl.when(to_m != m)
                def _():
                    copy.start()

        if 0 in steps:
            sent.count += lines - per // 2

    order = (1 - core, 3 - core, core, 2 + core)

    def collect(h):
        arrival(R.sized, n_mp * per - per // 2, R.r_recv.at[h], at.partner).wait_recv()
        for p, t in enumerate(order):
            R.features[h, p * rows : (p + 1) * rows, :] = jnp.concatenate(
                [R.blocks[h, t, j] for j in range(per)], axis=1
            )

    def inverse_of(h):
        arrival(R.sized_squares, n - 1, R.sq_sems.at[h], at.partner).wait_recv()
        return row_to_column(lax.rsqrt(jnp.sum(R.squares[h], axis=0) / D + eps))

    chunks = []
    for c, (h, first, last) in enumerate(bounds):
        kept, s1_out, s1_in, s2_out, s2_in, act = (
            getattr(R, f"{name}{c}") for name in ("kept", "s1_out", "s1_in", "s2_out", "s2_in", "act")
        )
        sem = lambda k, c=c: R.c_sems.at[c, k]
        chunks.append(
            dict(
                half=h, first=first, last=last, kept=kept, s1_out=s1_out, s1_in=s1_in,
                s2_out=s2_out, s2_in=s2_in, act=act,
                s1=push(s1_out, s1_in, sem(0), sem(1), at.sibling),
                s2=push(s2_out, s2_in, sem(0), sem(2), at.across),
                near=push(act.at[m], act.at[m], sem(0), sem(3), at.sibling),
                far=push(act.at[m], act.at[m], sem(0), sem(4), at.across),
                relay=push(
                    act.at[at.across[1]], act.at[at.across[1]], sem(0), sem(5), at.sibling
                ),
                sent=Sent(sem(0), getattr(R, f"sized{c}"), at.partner),
            )
        )
    halves = [[ch for ch in chunks if ch["half"] == h] for h in range(HALVES)]

    def multiply(ch):
        for g, weight in enumerate((R.gate_w, R.up_w)):
            product = times_transposed(R.features[ch["half"]], weight[ch["first"] : ch["last"], :])
            for p in range(2):
                ch["s1_out"][g, p] = product[p * rows : (p + 1) * rows].astype(bf16)
                ch["kept"][g, p] = product[(p + 2) * rows : (p + 3) * rows]
        ch["s1"].start()

    def pair_sum(ch):
        ch["s1"].wait_recv()
        for g in range(2):
            ch["s2_out"][g] = (
                ch["kept"][g, 1 - y] + ch["s1_in"][g, 1 - y].astype(f32)
            ).astype(bf16)
        ch["s2"].start()

    def activate(ch, inverse):
        ch["s2"].wait_recv()
        gate, up = [
            (ch["kept"][g, y] + ch["s1_in"][g, y].astype(f32) + ch["s2_in"][g].astype(f32))
            * inverse
            for g in range(2)
        ]
        ch["act"][m] = (gate / (1.0 + jnp.exp(-gate)) * up).astype(bf16)
        ch["far"].start()
        ch["near"].start()

    def pass_on(ch):
        ch["far"].wait_recv()
        ch["relay"].start()

    def down(ch):
        h, own = ch["half"], halves[ch["half"]]
        ch["near"].wait_recv()
        ch["relay"].wait_recv()
        act = ch["act"][...].reshape(n_mp * rows, ch["last"] - ch["first"])
        total = jnp.dot(act, R.down_w[ch["first"] : ch["last"], :], preferred_element_type=f32)
        if ch is not own[0]:
            total = R.acc[h] + total
        if ch is not own[-1]:
            R.acc[h] = total
            return
        for t in range(n_mp):
            for k in range(per):
                R.down_out[h, t, k % 2, k // 2] = total[
                    t * rows : (t + 1) * rows, k * width : (k + 1) * width
                ].astype(bf16)

    def leave(h):
        for i in range(n_mp):
            for b in range(2):
                if i == 0 and b == 0:
                    R.home_in[h, lo, m] = R.down_out[h, m, lo]
                    continue
                to_m, to_lo = lax.rem(m + i, n_mp), lax.rem(lo + b, 2)
                copy = push(
                    R.down_out.at[h, to_m, to_lo], R.home_in.at[h, lo, m], sent.sem,
                    R.h_sems.at[h, i], at.near(b, to_m),
                )
                sent.start(copy, per // 2)


    def send_home(h):
        for i in range(n_mp):
            source = lax.rem(m + n_mp - i, n_mp)
            blocks = (2 if i else 1) * (per // 2)
            arrival(R.sized, blocks, R.h_sems.at[h, i], at.partner).wait_recv()
            for k in range(per // 2):
                line = source * (per // 2) + k
                total = R.home_in[h, 0, source, k].astype(f32) + R.home_in[h, 1, source, k].astype(f32)
                R.home_out[h, line] = total.astype(bf16)
                copy = push(
                    R.home_out.at[h, line], R.terms.at[h, hi], sent.sem, R.t_recv.at[h],
                    (line * 2 + lo, m),
                )

                @pl.when(line == hi)
                def _():
                    R.terms[h, hi] = R.home_out[h, line]

                @pl.when(line != hi)
                def _():
                    copy.start()

        sent.count += lines - 1

    def conclude(h):
        arrival(R.sized, lines - 1, R.t_recv.at[h], at.partner).wait_recv()
        result = R.residual[part(h), :]
        for i in range(lines):
            result = result + R.terms[h, i].astype(f32)
        R.result[part(h), :] = result.astype(bf16)
        copy = pltpu.make_async_copy(
            R.result.at[pl.ds(h * rows, rows)], R.out.at[pl.ds(h * rows, rows)], R.o_sems.at[1, h]
        )
        copy.start()
        written.append(copy)

    loads["keys"].wait()
    loads["values"].wait()
    waiting = []
    for h in range(HALVES):
        for j in range(KV_HEADS):
            asked[h].take(j)
            attend(h, j)
            if h == 0 and j == 0:
                asked[0].hand_all()
            elif h + 1 < HALVES and lines == KV_HEADS:
                asked[h + 1].hand(j)
            waiting.append((h, j))
            if len(waiting) > LAG:
                join(*waiting.pop(0))
        if h + 1 < HALVES:
            asked[h + 1].hand_all()
    for item in waiting:
        join(*item)
    for g in range(KV_HEADS):
        loads[f"w_out{g}"].wait()
    loads["gain_ffn"].wait()
    answered = [Gather(at, R.att.at[h], R.a_sems.at[h], sent) for h in range(HALVES)]
    for h in range(HALVES):
        merge(h)
        answered[h].start()
    first, second = halves
    answered[0].hand_all()
    project(0, answered[0])
    answered[1].hand_all()
    project(1, answered[1])
    loads["gate"].wait()
    loads["up"].wait()
    later = range(1, lines)
    relay(0, later)
    collect(0)
    multiply(first[0])
    relay(1, later)
    pair_sum(first[0])
    for ch in first[1:]:
        multiply(ch)
        pair_sum(ch)
    inverse = [inverse_of(0)]
    collect(1)
    loads["down"].wait()
    for k, ch in enumerate(second):
        multiply(ch)
        activate(first[k], inverse[0])
        pair_sum(ch)
    inverse.append(inverse_of(1))
    for k, ch in enumerate(second):
        pass_on(first[k])
        down(first[k])
        activate(ch, inverse[1])
    leave(0)
    for ch in second:
        pass_on(ch)
        down(ch)
    leave(1)
    send_home(0)
    send_home(1)
    for h in range(HALVES):
        conclude(h)

    for copy in written:
        copy.wait()
    for record in (sent, sent_stats, sent_squares):
        record.wait()
    for ch in chunks:
        ch["sent"].count = 9
        ch["sent"].wait()


def layer(n, n_mp, *arrays):
    tokens, w_query, keys, w_gate, w_down = (arrays[i] for i in (0, 2, 4, 8, 10))
    rows, width = tokens.shape[0], w_query.shape[0]
    hidden, quarter = w_gate.shape
    lines, per = n // 2, n // n_mp
    bounds = []
    for h in range(HALVES):
        cuts = [min(hidden, -(-int(hidden * cut) // 128) * 128) for cut in CUTS[h]] + [hidden]
        bounds += [(h, first, last) for first, last in zip([0] + cuts, cuts) if first < last]
    part = rows // HALVES
    bf16, f32, dma = jnp.bfloat16, jnp.float32, pltpu.SemaphoreType.DMA
    scratch = dict(
        tokens=VMEM(tokens.shape, bf16),
        gain_attn=VMEM((D,), f32),
        bias=VMEM((1, width), f32),
        gain_ffn=VMEM((1, width), f32),
        w_query=VMEM(w_query.shape, bf16),
        keys=VMEM(keys.shape, bf16),
        values=VMEM(keys.shape, bf16),
        w_out=VMEM((KV_HEADS, width, D // KV_HEADS), bf16),
        gate_w=VMEM(w_gate.shape, bf16),
        up_w=VMEM(w_gate.shape, bf16),
        down_w=VMEM(w_down.shape, bf16),
        own_tokens=VMEM((rows, width), f32),
        residual=VMEM((rows, width), f32),
        qbuf=VMEM((HALVES, n, part, width), bf16),
        part_out=VMEM((HALVES, KV_HEADS, 2, n // KV_HEADS // 2, part, width), bf16),
        pair_in=VMEM((HALVES, KV_HEADS, n // KV_HEADS // 2, part, width), bf16),
        line_out=VMEM((HALVES, KV_HEADS, n // KV_HEADS // 2, part, width), bf16),
        part_in=VMEM((HALVES, lines, part, width), bf16),
        stat_out=VMEM((HALVES, KV_HEADS, 2 * SUM_ROW, part), f32),
        pair_stat=VMEM((HALVES, KV_HEADS, 2 * SUM_ROW, part), f32),
        line_stat=VMEM((HALVES, KV_HEADS, 2 * SUM_ROW, part), f32),
        stat_in=VMEM((HALVES, lines, 2 * SUM_ROW, part), f32),
        result=VMEM((rows, width), bf16),
        att=VMEM((HALVES, n, part, width), bf16),
        lined=VMEM((HALVES, lines, part, width), bf16),
        squares=VMEM((HALVES, n, 1, part), f32),
        blocks=VMEM((HALVES, n_mp, per, part, width), bf16),
        features=VMEM((HALVES, n_mp * part, quarter), bf16),
        acc=VMEM((HALVES, n_mp * part, w_down.shape[1]), f32),
        down_out=VMEM((HALVES, n_mp, 2, per // 2, part, width), bf16),
        home_in=VMEM((HALVES, 2, n_mp, per // 2, part, width), bf16),
        home_out=VMEM((HALVES, lines, part, width), bf16),
        terms=VMEM((HALVES, lines, part, width), bf16),
        sized=VMEM((HALVES * 8 * n, part, width), bf16),
        sized_stats=VMEM((HALVES * 2 * n, 2 * SUM_ROW, part), f32),
        sized_squares=VMEM((HALVES * n, 1, part), f32),
        w_sems=dma((10 + KV_HEADS,)),
        s_sems=dma((3,)),
        q_sems=dma((HALVES, 2, lines)),
        a_sems=dma((HALVES, 2, lines)),
        p_sems=dma((HALVES, 2, KV_HEADS)),
        m_recv=dma((HALVES, 2)),
        o_sems=dma((2, HALVES)),
        l_sems=dma((HALVES, lines)),
        sq_sems=dma((HALVES,)),
        r_recv=dma((HALVES,)),
        h_sems=dma((HALVES, n_mp)),
        t_recv=dma((HALVES,)),
        c_sems=dma((len(bounds), 6)),
    )
    for c, (_, first, last) in enumerate(bounds):
        span = last - first
        scratch[f"kept{c}"] = VMEM((2, 2, part, span), f32)
        scratch[f"s1_out{c}"] = VMEM((2, 2, part, span), bf16)
        scratch[f"s1_in{c}"] = VMEM((2, 2, part, span), bf16)
        scratch[f"s2_out{c}"] = VMEM((2, part, span), bf16)
        scratch[f"s2_in{c}"] = VMEM((2, part, span), bf16)
        scratch[f"sized{c}"] = VMEM((9, part, span), bf16)
        scratch[f"act{c}"] = VMEM((n_mp, part, span), bf16)
    names = ARGS + OUTS + tuple(scratch)
    block = jax.ShapeDtypeStruct((rows, width), bf16)
    anywhere = pl.BlockSpec(memory_space=pl.ANY)
    return pl.pallas_call(
        functools.partial(layer_kernel, n, n_mp, bounds, names),
        out_shape=(block, block),
        in_specs=[anywhere] * len(ARGS),
        out_specs=(anywhere, anywhere),
        scratch_shapes=list(scratch.values()),
        compiler_params=pltpu.CompilerParams(
            collective_id=1, has_side_effects=True, vmem_limit_bytes=60 * 2**20
        ),
        name="layer",
    )(*arrays)


def results_kernel(attended, out, attended_out, layer_out, held, sems):
    pairs = ((attended, attended_out), (out, layer_out))
    into = [pltpu.make_async_copy(src, held.at[i], sems.at[0, i]) for i, (src, _) in enumerate(pairs)]
    back = [pltpu.make_async_copy(held.at[i], dst, sems.at[1, i]) for i, (_, dst) in enumerate(pairs)]
    for copy in into:
        copy.start()
    for copy, onward in zip(into, back):
        copy.wait()
        onward.start()
    for copy in back:
        copy.wait()


def results(attended, out):
    anywhere = pl.BlockSpec(memory_space=pl.ANY)
    block = jax.ShapeDtypeStruct(out.shape, out.dtype)
    return pl.pallas_call(
        results_kernel,
        out_shape=(block, block),
        in_specs=[anywhere, anywhere],
        out_specs=(anywhere, anywhere),
        scratch_shapes=[VMEM((2,) + out.shape, out.dtype), pltpu.SemaphoreType.DMA((2, 2))],
        name="results",
    )(attended, out)


def body(
    n_seq,
    n_mp,
    tokens,
    gain_attn,
    w_query,
    query_bias,
    cache_keys,
    cache_values,
    w_out,
    gain_ffn,
    w_gate,
    w_up,
    w_down,
):
    attended, out = layer(
        n_seq,
        n_mp,
        tokens,
        gain_attn,
        w_query.T,
        query_bias[None, :],
        cache_keys,
        cache_values,
        w_out.T,
        gain_ffn[None, :],
        w_gate.T,
        w_up.T,
        w_down,
    )
    return results(attended, out)


def solution(mesh):
    placed = (
        P("mp", None),
        P(),
        P(None, "seq"),
        P("seq"),
        P(None, "seq", None),
        P(None, "seq", None),
        P(None, "seq"),
        P("seq"),
        P("mp", "seq"),
        P("mp", "seq"),
        P("seq", "mp"),
    )
    return jax.shard_map(
        functools.partial(body, mesh.shape["seq"], mesh.shape["mp"]),
        mesh=mesh,
        in_specs=placed,
        out_specs=(P("mp", "seq"), P("mp", "seq")),
        check_vma=False,
    )
```

time: 107 us -> 83.9 us (0.78)
  Pallas kernels: 101 us -> 83 us
  local copies, waits for them, and re-layouts: 4.27 us -> 0 us
    pallas_call x1, Pallas kernels: 101 us -> 81.4 us  [layer(): pl.pallas_call(functools.partial(layer_kernel, n, n_mp, bounds, names), o...]
    unnamed x2 -> x0, local copies, waits for them, and re-layouts: 2.95 us -> none
    pallas_call x0 -> x1, Pallas kernels: none -> 1.53 us  [results(): pl.pallas_call(results_kernel, out_shape=(block, block), in_specs=[anywhe...]
    broadcast_in_dim x1 -> x0, local copies, waits for them, and re-layouts: 1.33 us -> none  [body(): gain_attn[None, :]]
where the time goes in v2:
time: 83.9 us; the launch traced here: 83.8 us
  Pallas kernels  83 us (99%)
    pallas_call x1, Pallas kernels, layer(): pl.pallas_call(functools.partial(layer_kernel, n, n_mp, bounds, names), o...  81.4 us

profile of v2, /device:TPU:5, one launch (start us, length us, event | category | flops | bytes accessed | tf_op | source)
XLA Modules:
  0.0 83.8 jit_solution(3453572959861680778)
XLA Ops:
  0.6 81.4 %layer.1 = (bf16[64,448]{1,0:T(8,128)(2,1)}, bf16[64,448]{1,0:T(8,128)(2,1)}) custom-call(bf16[64,3584]{1,0:T(8,128)(2,1)} %refs_0_.1, f32[3584]{0:T(1024)} %refs_1_.1, bf16[448,3584]{1,0:T(8,128)(2,1)} %bitcast.8, f32[1,448]{1,0:T(1,128)} %bitcast.10, bf16[4,1024,128]{2,1,0:T(8,128)(2,1)} %refs_4_.1, bf16[4,1024,128]{2,1,0:T(8,128)(2,1)} %refs_5_.1, ...), custom_call_target="tpu_custom_call" | custom-call | tf_op jit(solution)/shard_map/layer/pallas_call | solution.py:645
  82.1 1.5 %results.1 = (bf16[64,448]{1,0:T(8,128)(2,1)}, bf16[64,448]{1,0:T(8,128)(2,1)}) custom-call(bf16[64,448]{1,0:T(8,128)(2,1)} %get-tuple-element.4.attended, bf16[64,448]{1,0:T(8,128)(2,1)} %get-tuple-element.5.out), custom_call_target="tpu_custom_call" | custom-call | tf_op jit(solution)/shard_map/results/pallas_call | solution.py:674

commit v3 on v2

v3 whole, which is shorter than its diff:
```python
import functools
import math
import types

import jax
import jax.numpy as jnp
from jax import lax
from jax.experimental import pallas as pl
from jax.experimental.pallas import tpu as pltpu
from jax.sharding import PartitionSpec as P

D = 3584
HEADS = 28
KV_HEADS = 4
HEAD = 128
GROUP = HEADS // KV_HEADS
SUM_ROW = 8
CUTS = ((0.3, 0.65), (0.45, 0.82))
PARTS = 2
ROWS = (0.5, 0.5)
LAG = 2
FORWARD = (False, False)
ASK_STRAIGHT = (True, False)
ANSWER_STRAIGHT = (False, False)

eps = 1e-06
EXP2_SCALE = HEAD ** (-0.5) * math.log2(math.e)
MESH = pl.DeviceIdType.MESH
VMEM = pltpu.VMEM
ARGS = (
    "tokens_hbm", "gain_attn_hbm", "w_query_hbm", "bias_hbm", "keys_hbm", "values_hbm",
    "w_out_hbm", "gain_ffn_hbm", "gate_hbm", "up_hbm", "down_hbm",
)
OUTS = ("attended", "out")


def push(src, dst, send, recv, to):
    return pltpu.make_async_remote_copy(
        src_ref=src,
        dst_ref=dst,
        send_sem=send,
        recv_sem=recv,
        device_id=to,
        device_id_type=MESH,
    )


def times_transposed(a, b):
    return lax.dot_general(a, b, (((1,), (1,)), ((), ())), preferred_element_type=jnp.float32)


def row_to_column(row):
    k = row.shape[1]
    across = lax.broadcasted_iota(jnp.int32, (k, k), 1)
    down = lax.broadcasted_iota(jnp.int32, (k, k), 0)
    return jnp.sum(jnp.where(across == down, row, 0.0), axis=1, keepdims=True)


def column_to_row(column):
    k = column.shape[0]
    across = lax.broadcasted_iota(jnp.int32, (k, k), 1)
    down = lax.broadcasted_iota(jnp.int32, (k, k), 0)
    return jnp.sum(jnp.where(across == down, column, 0.0), axis=0, keepdims=True)


def part_rows(rows):
    sizes = [int(rows * share) for share in ROWS]
    return [sum(sizes[:h]) for h in range(PARTS)], sizes


class Place:
    def __init__(self, n, n_mp):
        self.n, self.n_mp = n, n_mp
        self.lines, self.per, self.wide = n // 2, n // n_mp, n // KV_HEADS
        self.s, self.m = lax.axis_index("seq"), lax.axis_index("mp")
        self.hi, self.lo = self.s // 2, lax.rem(self.s, 2)
        self.y, self.core = self.m // 2, lax.rem(self.m, 2)
        self.partner = (self.hi * 2 + 1 - self.lo, self.m)
        self.sibling = (self.s, self.y * 2 + (1 - self.core))
        self.across = (self.s, (1 - self.y) * 2 + self.core)

    def ahead(self, d):
        return lax.rem(self.hi + d, self.lines)

    def behind(self, d):
        return lax.rem(self.hi + self.lines - d, self.lines)

    def near(self, b, m):
        return (self.hi * 2 + lax.rem(self.lo + b, 2), m)

    def group(self, j):
        return lax.rem(self.s // self.wide + KV_HEADS - j, KV_HEADS)


def greet(at):
    barrier = pltpu.get_barrier_semaphore()
    peers = [(lax.rem(at.s + d, at.n), at.m) for d in range(1, at.n)]
    peers += [
        at.near(b, lax.rem(at.m + i, at.n_mp)) for i in range(1, at.n_mp) for b in range(2)
    ]
    for peer in peers:
        pl.semaphore_signal(barrier, inc=1, device_id=peer, device_id_type=MESH)
    return lambda: pl.semaphore_wait(barrier, len(peers))


class Gather:
    def __init__(self, at, buf, sems, sent, straight):
        self.at, self.buf, self.sems, self.sent = at, buf, sems, sent
        self.straight = straight
        self.direct = [
            push(
                buf.at[at.s], buf.at[at.s], sent.sem, sems.at[d - 1],
                (at.ahead(d) * 2 + at.lo, at.m),
            )
            for d in range(1, at.lines)
        ]
        self.handed, self.taken = [], 0

    def start(self):
        at = self.at
        for copy in self.direct:
            copy.start()
            self.sent.count += 1
        self.hand(0)
        for d in range(1, at.lines if self.straight else 1):
            copy = push(
                self.buf.at[at.s], self.buf.at[at.s], self.sent.sem,
                self.sems.at[at.lines - 1 + d], (at.ahead(d) * 2 + 1 - at.lo, at.m),
            )

            @pl.when(at.core == 0)
            def _():
                copy.start()


    def hand(self, d):
        at = self.at
        if d < len(self.handed):
            return
        if d:
            self.direct[d - 1].wait_recv()
        block = self.buf.at[at.behind(d) * 2 + at.lo]
        copy = push(block, block, self.sent.sem, self.sems.at[at.lines - 1 + d], at.partner)
        if d and self.straight:

            @pl.when(at.core != 0)
            def _():
                copy.start()

        else:
            copy.start()
        self.handed.append(copy)
        self.sent.count += 1

    def hand_all(self):
        for d in range(self.at.lines):
            self.hand(d)

    def take(self, j):
        last = j if self.at.lines == KV_HEADS else self.at.lines - 1
        while self.taken <= last:
            self.hand(self.taken)
            self.handed[self.taken].wait_recv()
            self.taken += 1


class Sent:
    def __init__(self, sem, sized, to):
        self.sem, self.sized, self.to, self.count = sem, sized, to, 0

    def start(self, copy, blocks=1):
        copy.start()
        self.count += blocks

    def wait(self):
        of = self.sized.at[pl.ds(0, self.count)]
        push(of, of, self.sem, self.sem, self.to).wait_send()


def arrival(sized, count, sem, source):
    of = sized.at[pl.ds(0, count)]
    return push(of, of, sem, sem, source)


def layer_kernel(n, n_mp, bounds, per_part, names, *refs):
    R = types.SimpleNamespace(**dict(zip(names, refs)))
    at = Place(n, n_mp)
    s, m, hi, lo, y, core = at.s, at.m, at.hi, at.lo, at.y, at.core
    per, wide, lines = at.per, at.wide, at.lines
    width = R.out.shape[1]
    for name in per_part:
        setattr(R, name, [getattr(R, f"{name}_{h}") for h in range(PARTS)])
    bf16, f32 = jnp.bfloat16, jnp.float32
    starts, sizes = part_rows(R.out.shape[0])
    sent, sent_stats, sent_squares = (
        [Sent(R.s_sems.at[k, h], sized[h], at.partner) for h in range(PARTS)]
        for k, sized in enumerate((R.sized, R.sized_stats, R.sized_squares))
    )

    def part(h):
        return slice(starts[h], starts[h] + sizes[h])

    loads = {}
    slots = iter(range(R.w_sems.shape[0]))

    def load(name, src, dst):
        loads[name] = pltpu.make_async_copy(src, dst, R.w_sems.at[next(slots)])
        loads[name].start()

    load("tokens", R.tokens_hbm, R.tokens)
    load("gain_attn", R.gain_attn_hbm, R.gain_attn)
    load("bias", R.bias_hbm, R.bias)
    span = D // KV_HEADS
    for g in range(KV_HEADS):
        load(f"w_query{g}", R.w_query_hbm.at[:, pl.ds(g * span, span)], R.w_query.at[g])
    load("gain_ffn", R.gain_ffn_hbm, R.gain_ffn)
    everyone_here = greet(at)

    loads["tokens"].wait()
    hidden_in = R.tokens[...].astype(f32)
    mean_sq = jnp.sum(hidden_in * hidden_in, axis=1, keepdims=True) / D
    loads["gain_attn"].wait()
    normed = (hidden_in * lax.rsqrt(mean_sq + eps) * R.gain_attn[...].reshape(1, D)).astype(bf16)
    loads["bias"].wait()
    total = R.bias[...]
    for g in range(KV_HEADS):
        loads[f"w_query{g}"].wait()
        if g == KV_HEADS - 1:
            load("keys", R.keys_hbm, R.keys)
            load("values", R.values_hbm, R.values)
        total = total + times_transposed(normed[:, g * span : (g + 1) * span], R.w_query[g])
    queries = total.astype(bf16)
    for h in range(PARTS):
        R.qbuf[h][s] = queries[part(h)]
    everyone_here()
    asked = [Gather(at, R.qbuf[h], R.q_sems.at[h], sent[h], ASK_STRAIGHT[h]) for h in range(PARTS)]
    for flow in asked:
        flow.start()
    for g in range(KV_HEADS):
        load(f"w_out{g}", R.w_out_hbm.at[:, pl.ds(g * span, span)], R.w_out.at[g])
    load("gate", R.gate_hbm, R.gate_w)
    load("up", R.up_hbm, R.up_w)
    load("down", R.down_hbm, R.down_w)
    for k in range(n):

        @pl.when(s == k)
        def _():
            R.own_tokens[...] = R.tokens[:, k * width : (k + 1) * width].astype(f32)

    def attend(h, j):
        g, rows = at.group(j), sizes[h]
        heads = [slice(i * rows, (i + 1) * rows) for i in range(GROUP)]
        q = jnp.concatenate([R.qbuf[h][g * wide + i] for i in range(wide)], axis=1)
        stacked = jnp.concatenate([q[:, i * HEAD : (i + 1) * HEAD] for i in range(GROUP)], axis=0)
        scores = times_transposed(stacked, R.keys[g])
        highest = jnp.max(scores, axis=1, keepdims=True)
        probs = jnp.exp2((scores - highest) * EXP2_SCALE)
        sums = jnp.sum(probs, axis=1, keepdims=True)
        weighted = jnp.dot(probs.astype(bf16), R.values[g], preferred_element_type=f32)
        side = jnp.concatenate([weighted[head] for head in heads], axis=1).astype(bf16)
        for i in range(wide):
            R.part_out[h][j, i % 2, i // 2] = side[:, i * width : (i + 1) * width]
        R.stat_out[h][j] = jnp.zeros((2 * SUM_ROW, rows), f32)
        for i in range(GROUP):
            R.stat_out[h][j, i : i + 1, :] = column_to_row(highest[heads[i]] * EXP2_SCALE)
            R.stat_out[h][j, i + SUM_ROW : i + SUM_ROW + 1, :] = column_to_row(sums[heads[i]])
        for src, dst, k, record, blocks in (
            (R.part_out[h].at[j, 1 - lo], R.pair_in[h].at[j], 0, sent[h], wide // 2),
            (R.stat_out[h].at[j], R.pair_stat[h].at[j], 1, sent_stats[h], 1),
        ):
            copy = push(src, dst, record.sem, R.p_sems.at[h, k, j], at.partner)
            record.start(copy, blocks)
            paired[h, j].append(copy)

    paired = {(h, j): [] for h in range(PARTS) for j in range(KV_HEADS)}
    index = lax.rem(lax.broadcasted_iota(jnp.int32, (2 * SUM_ROW, width), 0), SUM_ROW)
    picks = []
    for k in range(wide // 2):
        first = (k * 2 + lo) * width
        column = first + lax.broadcasted_iota(jnp.int32, (2 * SUM_ROW, width), 1)
        picks.append(jnp.where(lax.div(column, HEAD) == index, 1.0, 0.0).astype(bf16))

    def spread(factor, pick):
        coarse = factor.astype(bf16).astype(f32)
        pair = jnp.concatenate([coarse, factor - coarse], axis=0).astype(bf16)
        return lax.dot_general(pair, pick, (((0,), (0,)), ((), ())), preferred_element_type=f32)

    def join(h, j):
        for copy in paired[h, j]:
            copy.wait_recv()
        mine, other = R.stat_out[h][j], R.pair_stat[h][j]
        top = jnp.maximum(mine[:SUM_ROW], other[:SUM_ROW])
        scale, scale_other = jnp.exp2(mine[:SUM_ROW] - top), jnp.exp2(other[:SUM_ROW] - top)
        R.line_stat[h][j, :SUM_ROW, :] = top
        R.line_stat[h][j, SUM_ROW:, :] = mine[SUM_ROW:] * scale + other[SUM_ROW:] * scale_other
        g = at.group(j)
        for k in range(wide // 2):
            total = R.part_out[h][j, lo, k].astype(f32) * spread(scale, picks[k]) + R.pair_in[h][j, k].astype(f32) * spread(scale_other, picks[k])
            R.line_out[h][j, k] = total.astype(bf16)
            line = g * (wide // 2) + k
            if wide // 2 == 1 and j == 0:
                R.part_in[h][hi] = R.line_out[h][j, k]
                R.stat_in[h][hi] = R.line_stat[h][j]
                continue
            for src, dst, kind, record in (
                (R.line_out[h].at[j, k], R.part_in[h].at[hi], 0, sent[h]),
                (R.line_stat[h].at[j], R.stat_in[h].at[hi], 1, sent_stats[h]),
            ):
                copy = push(src, dst, record.sem, R.m_recv.at[h, kind], (line * 2 + lo, m))
                if j:
                    record.start(copy)
                    continue

                @pl.when(line != hi)
                def _():
                    copy.start()

                record.count += int(k > 0)
            if j == 0:

                @pl.when(line == hi)
                def _():
                    R.part_in[h][hi] = R.line_out[h][j, k]
                    R.stat_in[h][hi] = R.line_stat[h][j]

    def merge(h):
        rows = sizes[h]
        arrival(R.sized[h], lines - 1, R.m_recv.at[h, 0], at.partner).wait_recv()
        arrival(R.sized_stats[h], lines - 1, R.m_recv.at[h, 1], at.partner).wait_recv()
        maxima, sums = R.stat_in[h][:, :SUM_ROW, :], R.stat_in[h][:, SUM_ROW:, :]
        rescale = jnp.exp2(maxima - jnp.max(maxima, axis=0, keepdims=True))
        total = jnp.sum(sums * rescale, axis=0)
        row = lax.broadcasted_iota(jnp.int32, (SUM_ROW, rows), 0)
        inverse = 1.0 / jnp.where(row < GROUP, total, 1.0)
        column = lax.rem(s, wide) * width + lax.broadcasted_iota(
            jnp.int32, (2 * SUM_ROW, width), 1
        )
        pick = jnp.where(lax.div(column, HEAD) == index, 1.0, 0.0).astype(bf16)
        result = jnp.zeros((rows, width), f32)
        for i in range(lines):
            result = result + R.part_in[h][i].astype(f32) * spread(rescale[i] * inverse, pick)
        R.att[h][s] = result.astype(bf16)
        copy = pltpu.make_async_copy(R.att[h].at[s], R.attended.at[pl.ds(starts[h], rows)], R.o_sems.at[0])
        copy.start()


    def project(h, flow):
        total = R.own_tokens[part(h), :]
        for j in range(KV_HEADS):
            flow.take(j)
            g = at.group(j)
            block = jnp.concatenate([R.att[h][g * wide + i] for i in range(wide)], axis=1)
            total = total + times_transposed(block, R.w_out[g])
        R.residual[part(h), :] = total
        R.lined[h][hi] = (total * R.gain_ffn[...]).astype(bf16)
        R.squares[h][s] = column_to_row(jnp.sum(total * total, axis=1, keepdims=True))
        for d in range(1, lines):
            copy = push(
                R.lined[h].at[hi], R.lined[h].at[hi], sent[h].sem, R.l_sems.at[h, d - 1],
                (at.ahead(d) * 2 + lo, m),
            )
            sent[h].start(copy)
            lined[h].append(copy)
        relay(h, range(1))
        for d in range(1, n):
            copy = push(
                R.squares[h].at[s], R.squares[h].at[s], sent_squares[h].sem, R.sq_sems.at[h],
                (lax.rem(s + d, n), m),
            )
            sent_squares[h].start(copy)

    lined = [[] for _ in range(PARTS)]

    def relay(h, steps):
        for d in steps:
            if d:
                lined[h][d - 1].wait_recv()
            line = at.behind(d)
            source = line * 2 + lo
            to_m, k = source // per, lax.rem(source, per)
            for b in range(1 if FORWARD[h] else 2):
                copy = push(
                    R.lined[h].at[line], R.blocks[h].at[m, k], sent[h].sem, R.r_recv.at[h],
                    at.near(b, to_m),
                )
                if b:
                    sent[h].start(copy)
                    continue

                @pl.when(to_m == m)
                def _():
                    R.blocks[h][m, k] = R.lined[h][line]

                @pl.when(to_m != m)
                def _():
                    copy.start()

        if 0 in steps:
            sent[h].count += lines - per // 2

    order = (1 - core, 3 - core, core, 2 + core)

    def forward(h):
        if not FORWARD[h]:
            return
        arrival(R.sized[h], (n_mp - 1) * (per // 2), R.r_recv.at[h], at.partner).wait_recv()
        for k in range(per // 2):
            for t in range(n_mp):
                block = R.blocks[h].at[t, k * 2 + lo]
                copy = push(block, block, sent[h].sem, R.f_recv.at[h], at.partner)
                sent[h].start(copy)

    def collect(h):
        if FORWARD[h]:
            blocks = n_mp * (per // 2)
            arrival(R.sized[h], blocks, R.f_recv.at[h], at.partner).wait_recv()
        else:
            blocks = n_mp * per - per // 2
            arrival(R.sized[h], blocks, R.r_recv.at[h], at.partner).wait_recv()
        rows = sizes[h]
        for p, t in enumerate(order):
            R.features[h][p * rows : (p + 1) * rows, :] = jnp.concatenate(
                [R.blocks[h][t, j] for j in range(per)], axis=1
            )

    def inverse_of(h):
        arrival(R.sized_squares[h], n - 1, R.sq_sems.at[h], at.partner).wait_recv()
        return row_to_column(lax.rsqrt(jnp.sum(R.squares[h][...], axis=0) / D + eps))

    chunks = []
    for c, (h, first, last) in enumerate(bounds):
        kept, s1_out, s1_in, s2_out, s2_in, act = (
            getattr(R, f"{name}{c}") for name in ("kept", "s1_out", "s1_in", "s2_out", "s2_in", "act")
        )
        sem = lambda k, c=c: R.c_sems.at[c, k]
        chunks.append(
            dict(
                half=h, first=first, last=last, kept=kept, s1_out=s1_out, s1_in=s1_in,
                s2_out=s2_out, s2_in=s2_in, act=act,
                s1=push(s1_out, s1_in, sem(0), sem(1), at.sibling),
                s2=push(s2_out, s2_in, sem(0), sem(2), at.across),
                near=push(act.at[m], act.at[m], sem(0), sem(4), at.sibling),
                far=push(act.at[m], act.at[m], sem(0), sem(3), at.across),
                relay=push(
                    act.at[at.across[1]], act.at[at.across[1]], sem(0), sem(4), at.sibling
                ),
                both=arrival(getattr(R, f"chunk{c}"), 2, sem(4), at.sibling),
                sent=Sent(sem(0), getattr(R, f"chunk{c}"), at.partner),
            )
        )
    halves = [[ch for ch in chunks if ch["half"] == h] for h in range(PARTS)]

    def multiply(ch):
        for g, weight in enumerate((R.gate_w, R.up_w)):
            rows = sizes[ch["half"]]
            product = times_transposed(R.features[ch["half"]][...], weight[ch["first"] : ch["last"], :])
            for p in range(2):
                ch["s1_out"][g, p] = product[p * rows : (p + 1) * rows].astype(bf16)
                ch["kept"][g, p] = product[(p + 2) * rows : (p + 3) * rows]
        ch["s1"].start()

    def pair_sum(ch):
        ch["s1"].wait_recv()
        for g in range(2):
            ch["s2_out"][g] = (
                ch["kept"][g, 1 - y] + ch["s1_in"][g, 1 - y].astype(f32)
            ).astype(bf16)
        ch["s2"].start()

    def activate(ch, inverse):
        ch["s2"].wait_recv()
        gate, up = [
            (ch["kept"][g, y] + ch["s1_in"][g, y].astype(f32) + ch["s2_in"][g].astype(f32))
            * inverse
            for g in range(2)
        ]
        ch["act"][m] = (gate / (1.0 + jnp.exp(-gate)) * up).astype(bf16)
        ch["far"].start()
        ch["near"].start()

    def pass_on(ch):
        ch["far"].wait_recv()
        ch["relay"].start()

    def down(ch):
        h, own, rows = ch["half"], halves[ch["half"]], sizes[ch["half"]]
        ch["both"].wait_recv()
        act = ch["act"][...].reshape(n_mp * rows, ch["last"] - ch["first"])
        total = jnp.dot(act, R.down_w[ch["first"] : ch["last"], :], preferred_element_type=f32)
        if ch is not own[0]:
            total = R.acc[h][...] + total
        if ch is not own[-1]:
            R.acc[h][...] = total
            return
        for t in range(n_mp):
            for k in range(per):
                R.down_out[h][t, k % 2, k // 2] = total[
                    t * rows : (t + 1) * rows, k * width : (k + 1) * width
                ].astype(bf16)

    def leave(h):
        for i in range(n_mp):
            for b in range(2):
                if i == 0 and b == 0:
                    R.home_in[h][lo, m] = R.down_out[h][m, lo]
                    continue
                to_m, to_lo = lax.rem(m + i, n_mp), lax.rem(lo + b, 2)
                copy = push(
                    R.down_out[h].at[to_m, to_lo], R.home_in[h].at[lo, m], sent[h].sem,
                    R.h_sems.at[h, i], at.near(b, to_m),
                )
                sent[h].start(copy, per // 2)


    def send_home(h):
        for i in range(n_mp):
            source = lax.rem(m + n_mp - i, n_mp)
            blocks = (2 if i else 1) * (per // 2)
            arrival(R.sized[h], blocks, R.h_sems.at[h, i], at.partner).wait_recv()
            for k in range(per // 2):
                line = source * (per // 2) + k
                total = R.home_in[h][0, source, k].astype(f32) + R.home_in[h][1, source, k].astype(f32)
                R.home_out[h][line] = total.astype(bf16)
                copy = push(
                    R.home_out[h].at[line], R.terms[h].at[hi], sent[h].sem, R.t_recv.at[h],
                    (line * 2 + lo, m),
                )

                @pl.when(line == hi)
                def _():
                    R.terms[h][hi] = R.home_out[h][line]

                @pl.when(line != hi)
                def _():
                    copy.start()

        sent[h].count += lines - 1

    def conclude(h):
        arrival(R.sized[h], lines - 1, R.t_recv.at[h], at.partner).wait_recv()
        result = R.residual[part(h), :]
        for i in range(lines):
            result = result + R.terms[h][i].astype(f32)
        R.result[part(h), :] = result.astype(bf16)
        copy = pltpu.make_async_copy(
            R.result.at[pl.ds(starts[h], sizes[h])], R.out.at[pl.ds(starts[h], sizes[h])],
            R.o_sems.at[0],
        )
        copy.start()

    loads["keys"].wait()
    loads["values"].wait()
    waiting = []

    def score(h, j):
        asked[h].take(j)
        attend(h, j)
        waiting.append((h, j))
        if len(waiting) > LAG:
            join(*waiting.pop(0))

    answered = [Gather(at, R.att[h], R.a_sems.at[h], sent[h], ANSWER_STRAIGHT[h]) for h in range(PARTS)]

    def answer(h):
        merge(h)
        answered[h].start()

    score(0, 0)
    asked[0].hand_all()
    for h in range(PARTS):
        for j in range(KV_HEADS):
            if h or j:
                score(h, j)
            if h + 1 < PARTS and lines == KV_HEADS:
                asked[h + 1].hand(j)
        if h + 1 < PARTS:
            asked[h + 1].hand_all()
    for item in waiting[:-1]:
        join(*item)
    for g in range(KV_HEADS):
        loads[f"w_out{g}"].wait()
    loads["gain_ffn"].wait()
    answer(0)
    join(*waiting[-1])
    a, b = halves
    later = range(1, lines)
    answered[0].hand_all()
    answer(1)
    project(0, answered[0])
    answered[1].hand_all()
    relay(0, later)
    project(1, answered[1])
    loads["gate"].wait()
    loads["up"].wait()
    collect(0)
    multiply(a[0])
    relay(1, later)
    for before, ch in zip(a, a[1:]):
        multiply(ch)
        pair_sum(before)
    pair_sum(a[-1])
    inverse = [inverse_of(0)]
    loads["down"].wait()
    forward(1)
    activate(a[0], inverse[0])
    collect(1)
    multiply(b[0])
    inverse.append(inverse_of(1))
    for k, ch in enumerate(b[1:]):
        multiply(ch)
        pair_sum(b[k])
        if k + 1 < len(a):
            activate(a[k + 1], inverse[0])
    for ch in a[len(b) :]:
        activate(ch, inverse[0])
    pass_on(a[0])
    pair_sum(b[-1])
    for k, ch in enumerate(a):
        if k + 1 < len(a):
            pass_on(a[k + 1])
        down(ch)
        if k < len(b):
            activate(b[k], inverse[1])
    for ch in b[len(a) :]:
        activate(ch, inverse[1])
    leave(0)
    pass_on(b[0])
    for k, ch in enumerate(b):
        if k + 1 < len(b):
            pass_on(b[k + 1])
        down(ch)
    leave(1)
    for h in range(PARTS):
        send_home(h)
    for h in range(PARTS):
        conclude(h)

    pltpu.make_async_copy(R.sized_out, R.sized_out, R.o_sems.at[0]).wait()
    for record in sent + sent_stats + sent_squares:
        record.wait()
    for ch in chunks:
        ch["sent"].count = 9
        ch["sent"].wait()


def layer(n, n_mp, *arrays):
    tokens, w_query, keys, w_gate, w_down = (arrays[i] for i in (0, 2, 4, 8, 10))
    rows, width = tokens.shape[0], w_query.shape[0]
    hidden, quarter = w_gate.shape
    lines, per = n // 2, n // n_mp
    bounds = []
    for h in range(PARTS):
        cuts = [min(hidden, -(-int(hidden * cut) // 128) * 128) for cut in CUTS[h]] + [hidden]
        bounds += [(h, first, last) for first, last in zip([0] + cuts, cuts) if first < last]
    bf16, f32, dma = jnp.bfloat16, jnp.float32, pltpu.SemaphoreType.DMA
    scratch = dict(
        tokens=VMEM(tokens.shape, bf16),
        gain_attn=VMEM((D,), f32),
        bias=VMEM((1, width), f32),
        gain_ffn=VMEM((1, width), f32),
        w_query=VMEM((KV_HEADS, width, D // KV_HEADS), bf16),
        keys=VMEM(keys.shape, bf16),
        values=VMEM(keys.shape, bf16),
        w_out=VMEM((KV_HEADS, width, D // KV_HEADS), bf16),
        gate_w=VMEM(w_gate.shape, bf16),
        up_w=VMEM(w_gate.shape, bf16),
        down_w=VMEM(w_down.shape, bf16),
        sized_out=VMEM((2 * rows, width), bf16),
        own_tokens=VMEM((rows, width), f32),
        residual=VMEM((rows, width), f32),
        result=VMEM((rows, width), bf16),
        w_sems=dma((9 + 2 * KV_HEADS,)),
        s_sems=dma((3, PARTS)),
        q_sems=dma((PARTS, 2 * lines - 1)),
        a_sems=dma((PARTS, 2 * lines - 1)),
        p_sems=dma((PARTS, 2, KV_HEADS)),
        m_recv=dma((PARTS, 2)),
        o_sems=dma((1,)),
        l_sems=dma((PARTS, lines - 1)),
        sq_sems=dma((PARTS,)),
        r_recv=dma((PARTS,)),
        f_recv=dma((PARTS,)),
        h_sems=dma((PARTS, n_mp)),
        t_recv=dma((PARTS,)),
        c_sems=dma((len(bounds), 5)),
    )
    for h, part in enumerate(part_rows(rows)[1]):
        own = dict(
            qbuf=VMEM((n, part, width), bf16),
            part_out=VMEM((KV_HEADS, 2, n // KV_HEADS // 2, part, width), bf16),
            pair_in=VMEM((KV_HEADS, n // KV_HEADS // 2, part, width), bf16),
            line_out=VMEM((KV_HEADS, n // KV_HEADS // 2, part, width), bf16),
            part_in=VMEM((lines, part, width), bf16),
            stat_out=VMEM((KV_HEADS, 2 * SUM_ROW, part), f32),
            pair_stat=VMEM((KV_HEADS, 2 * SUM_ROW, part), f32),
            line_stat=VMEM((KV_HEADS, 2 * SUM_ROW, part), f32),
            stat_in=VMEM((lines, 2 * SUM_ROW, part), f32),
            att=VMEM((n, part, width), bf16),
            lined=VMEM((lines, part, width), bf16),
            squares=VMEM((n, 1, part), f32),
            blocks=VMEM((n_mp, per, part, width), bf16),
            features=VMEM((n_mp * part, quarter), bf16),
            acc=VMEM((n_mp * part, w_down.shape[1]), f32),
            down_out=VMEM((n_mp, 2, per // 2, part, width), bf16),
            home_in=VMEM((2, n_mp, per // 2, part, width), bf16),
            home_out=VMEM((lines, part, width), bf16),
            terms=VMEM((lines, part, width), bf16),
            sized=VMEM((8 * n, part, width), bf16),
            sized_stats=VMEM((2 * n, 2 * SUM_ROW, part), f32),
            sized_squares=VMEM((n, 1, part), f32),
        )
        scratch.update({f"{name}_{h}": ref for name, ref in own.items()})
    for c, (h, first, last) in enumerate(bounds):
        span, part = last - first, part_rows(rows)[1][h]
        buffers = dict(
            kept=VMEM((2, 2, part, span), f32),
            s1_out=VMEM((2, 2, part, span), bf16),
            s1_in=VMEM((2, 2, part, span), bf16),
            s2_out=VMEM((2, part, span), bf16),
            s2_in=VMEM((2, part, span), bf16),
            chunk=VMEM((9, part, span), bf16),
            act=VMEM((n_mp, part, span), bf16),
        )
        scratch.update({f"{name}{c}": ref for name, ref in buffers.items()})
    names = ARGS + OUTS + tuple(scratch)
    block = jax.ShapeDtypeStruct((rows, width), bf16)
    anywhere = pl.BlockSpec(memory_space=pl.ANY)
    return pl.pallas_call(
        functools.partial(layer_kernel, n, n_mp, bounds, tuple(own), names),
        out_shape=(block, block),
        in_specs=[anywhere] * len(ARGS),
        out_specs=(anywhere, anywhere),
        scratch_shapes=list(scratch.values()),
        compiler_params=pltpu.CompilerParams(
            collective_id=1, has_side_effects=True, vmem_limit_bytes=60 * 2**20
        ),
        name="layer",
    )(*arrays)


def results_kernel(attended, out, attended_out, layer_out, held, sems):
    pairs = ((attended, attended_out), (out, layer_out))
    into = [pltpu.make_async_copy(src, held.at[i], sems.at[0, i]) for i, (src, _) in enumerate(pairs)]
    back = [pltpu.make_async_copy(held.at[i], dst, sems.at[1, i]) for i, (_, dst) in enumerate(pairs)]
    for copy in into:
        copy.start()
    for copy, onward in zip(into, back):
        copy.wait()
        onward.start()
    for copy in back:
        copy.wait()


def results(attended, out):
    anywhere = pl.BlockSpec(memory_space=pl.ANY)
    block = jax.ShapeDtypeStruct(out.shape, out.dtype)
    return pl.pallas_call(
        results_kernel,
        out_shape=(block, block),
        in_specs=[anywhere, anywhere],
        out_specs=(anywhere, anywhere),
        scratch_shapes=[VMEM((2,) + out.shape, out.dtype), pltpu.SemaphoreType.DMA((2, 2))],
        name="results",
    )(attended, out)


def body(
    n_seq,
    n_mp,
    tokens,
    gain_attn,
    w_query,
    query_bias,
    cache_keys,
    cache_values,
    w_out,
    gain_ffn,
    w_gate,
    w_up,
    w_down,
):
    attended, out = layer(
        n_seq,
        n_mp,
        tokens,
        gain_attn,
        w_query.T,
        query_bias[None, :],
        cache_keys,
        cache_values,
        w_out.T,
        gain_ffn[None, :],
        w_gate.T,
        w_up.T,
        w_down,
    )
    return results(attended, out)


def solution(mesh):
    placed = (
        P("mp", None),
        P(),
        P(None, "seq"),
        P("seq"),
        P(None, "seq", None),
        P(None, "seq", None),
        P(None, "seq"),
        P("seq"),
        P("mp", "seq"),
        P("mp", "seq"),
        P("seq", "mp"),
    )
    return jax.shard_map(
        functools.partial(body, mesh.shape["seq"], mesh.shape["mp"]),
        mesh=mesh,
        in_specs=placed,
        out_specs=(P("mp", "seq"), P("mp", "seq")),
        check_vma=False,
    )
```

time: 83.9 us -> 80.6 us (0.961)
  Pallas kernels: 83 us -> 79.6 us
    pallas_call x1, Pallas kernels: 81.4 us -> 78 us  [layer(): pl.pallas_call(functools.partial(layer_kernel, n, n_mp, bounds, tuple(own...]
where the time goes in v3:
time: 80.6 us; the launch traced here: 80.4 us
  Pallas kernels  79.6 us (99%)
    pallas_call x1, Pallas kernels, layer(): pl.pallas_call(functools.partial(layer_kernel, n, n_mp, bounds, tuple(own...  78 us

profile of v3, /device:TPU:5, one launch (start us, length us, event | category | flops | bytes accessed | tf_op | source)
XLA Modules:
  0.0 80.4 jit_solution(7792133548868168227)
XLA Ops:
  0.6 78.0 %layer.1 = (bf16[64,448]{1,0:T(8,128)(2,1)}, bf16[64,448]{1,0:T(8,128)(2,1)}) custom-call(bf16[64,3584]{1,0:T(8,128)(2,1)} %refs_0_.1, f32[3584]{0:T(1024)} %refs_1_.1, bf16[448,3584]{1,0:T(8,128)(2,1)} %bitcast.8, f32[1,448]{1,0:T(1,128)} %bitcast.10, bf16[4,1024,128]{2,1,0:T(8,128)(2,1)} %refs_4_.1, bf16[4,1024,128]{2,1,0:T(8,128)(2,1)} %refs_5_.1, ...), custom_call_target="tpu_custom_call" | custom-call | tf_op jit(solution)/shard_map/layer/pallas_call | solution.py:728
  78.7 1.5 %results.1 = (bf16[64,448]{1,0:T(8,128)(2,1)}, bf16[64,448]{1,0:T(8,128)(2,1)}) custom-call(bf16[64,448]{1,0:T(8,128)(2,1)} %get-tuple-element.4.attended, bf16[64,448]{1,0:T(8,128)(2,1)} %get-tuple-element.5.out), custom_call_target="tpu_custom_call" | custom-call | tf_op jit(solution)/shard_map/results/pallas_call | solution.py:757
